TPU v7x, 32 devices: a 4x4x1 block of a 4x4x8 slice. The times are simulated.
32 devices in a mesh: dp: 1 (over z), cp: 32 (over y, x, core).
Axes of the slice: x: 4, y: 4, z: 1, core: 2. Of those that a mesh axis runs over, the one named last changes fastest.
The devices are a block of a 4x4x8 slice.
Arguments:
- hidden: bfloat16 [16384, 2560], P(('dp', 'cp'))
- w_query: bfloat16 [6, 2560, 8, 256], replicated
- w_key: bfloat16 [6, 2560, 4, 256], replicated
- w_value: bfloat16 [6, 2560, 4, 256], replicated
- w_out: bfloat16 [6, 8, 256, 2560], replicated
Outputs:
- output: bfloat16 [16384, 2560], P(('dp', 'cp'))
All inputs are finite; a program needn't handle non-finite values.
Results may differ from a plain program's by a relative error of at most 0.0117122.
Values are sent between devices in bfloat16 or wider.
A program may use at most 768 MiB of HBM per device.

v0:
```python
import jax
import jax.numpy as jnp
from jax import lax
from jax.sharding import PartitionSpec as P

WINDOW = 1024
EPS_NORM = 1e-6
NEG_BIG = -1e30


def rms_normed(rows_in):
    widened = rows_in.astype(jnp.float32)
    return widened * lax.rsqrt(jnp.mean(widened * widened, axis=-1, keepdims=True) + EPS_NORM)


def project_qkv(hidden, w_query, w_key, w_value):
    normed = rms_normed(hidden).astype(jnp.bfloat16)
    queries = jnp.einsum("td,dhe->the", normed, w_query, preferred_element_type=jnp.float32).astype(jnp.bfloat16)
    key_rows = jnp.einsum("td,dhe->the", normed, w_key, preferred_element_type=jnp.float32).astype(jnp.bfloat16)
    value_rows = jnp.einsum("td,dhe->the", normed, w_value, preferred_element_type=jnp.float32).astype(jnp.bfloat16)
    return queries, key_rows, value_rows


def residual_update(hidden, attn_out, w_out):
    update = jnp.einsum("the,hed->td", attn_out, w_out, preferred_element_type=jnp.float32)
    return (hidden.astype(jnp.float32) + rms_normed(update)).astype(jnp.bfloat16)


def window_attention(queries, key_rows, value_rows, query_pos, key_pos):
    num_rows, num_heads, head_dim = queries.shape
    kv_heads = key_rows.shape[1]
    grouped = queries.reshape(num_rows, kv_heads, num_heads // kv_heads, head_dim)
    scores = jnp.einsum("qhgd,khd->hgqk", grouped, key_rows, preferred_element_type=jnp.float32) * head_dim ** -0.5
    offsets = key_pos[None, :] - query_pos[:, None]
    allowed = (offsets <= 0) & (offsets > -WINDOW) & (key_pos[None, :] >= 0)
    scores = jnp.where(allowed, scores, NEG_BIG)
    row_max = jnp.max(scores, axis=-1, keepdims=True)
    weights = jnp.exp(scores - row_max)
    row_sum = jnp.sum(weights, axis=-1)
    attn_out = jnp.einsum("hgqk,khd->hgqd", weights.astype(jnp.bfloat16), value_rows, preferred_element_type=jnp.float32)
    attn_out = attn_out / row_sum[..., None]
    return jnp.transpose(attn_out, (2, 0, 1, 3)).reshape(num_rows, num_heads, head_dim).astype(jnp.bfloat16)


def gather_halo(key_rows, value_rows, num_dev):
    tok_rows = key_rows.shape[0]
    piece_len = min(WINDOW, tok_rows)
    num_hops = WINDOW // piece_len
    tail_kv = jnp.stack([key_rows[tok_rows - piece_len:], value_rows[tok_rows - piece_len:]])
    pieces = []
    for hop_dist in range(num_hops, 0, -1):
        if hop_dist < num_dev:
            perm_pairs = [(source, source + hop_dist) for source in range(num_dev - hop_dist)]
            pieces.append(lax.ppermute(tail_kv, "cp", perm_pairs))
        else:
            pieces.append(jnp.zeros_like(tail_kv))
    halo_kv = jnp.concatenate(pieces, axis=1)
    return halo_kv[0], halo_kv[1]


def local_attention(queries, key_rows, value_rows, halo_keys, halo_values, dev_rank):
    tok_rows = queries.shape[0]
    block_len = tok_rows // 2
    all_keys = jnp.concatenate([halo_keys, key_rows], axis=0)
    all_values = jnp.concatenate([halo_values, value_rows], axis=0)
    key_span = WINDOW + block_len
    outputs = []
    for half_idx in range(2):
        start_row = half_idx * block_len
        query_pos = dev_rank * tok_rows + start_row + jnp.arange(block_len)
        key_pos = dev_rank * tok_rows - WINDOW + start_row + jnp.arange(key_span)
        outputs.append(window_attention(
            queries[start_row:start_row + block_len],
            all_keys[start_row:start_row + key_span],
            all_values[start_row:start_row + key_span],
            query_pos, key_pos))
    return jnp.concatenate(outputs, axis=0)


def output_owner(block_idx, num_dev):
    return block_idx if block_idx < num_dev else 2 * num_dev - 1 - block_idx


def to_output_layout(hidden, dev_rank, num_dev):
    block_len = hidden.shape[0] // 2
    even_pairs = [(source, output_owner(2 * source, num_dev)) for source in range(num_dev)]
    odd_pairs = [(source, output_owner(2 * source + 1, num_dev)) for source in range(num_dev)]
    from_even = lax.ppermute(hidden[:block_len], "cp", even_pairs)
    from_odd = lax.ppermute(hidden[block_len:], "cp", odd_pairs)
    is_even = dev_rank % 2 == 0
    lead_rows = jnp.where(is_even, from_even, from_odd)
    trail_rows = jnp.where(is_even, from_odd, from_even)
    return jnp.concatenate([lead_rows, trail_rows], axis=0)


def causal_block_attention(queries, block_id, kv_all, num_dev):
    block_len, num_heads, head_dim = queries.shape
    kv_heads = kv_all.shape[-2]
    group_size = num_heads // kv_heads
    grouped = queries.reshape(block_len, kv_heads, group_size, head_dim)
    query_pos = block_id * block_len + jnp.arange(block_len)
    zero_idx = jnp.zeros((), jnp.int32)

    def kv_step(key_block, state_in):
        row_max, row_sum, acc_out = state_in
        in_front = key_block < num_dev
        owner_dev = jnp.where(in_front, key_block, 2 * num_dev - 1 - key_block)
        half_idx = jnp.where(in_front, 0, 1).astype(jnp.int32)
        kv_block = lax.dynamic_slice(
            kv_all, (owner_dev, zero_idx, half_idx, zero_idx, zero_idx, zero_idx),
            (1, 2, 1, block_len, kv_heads, head_dim)).reshape(2, block_len, kv_heads, head_dim)
        scores = jnp.einsum("qhgd,khd->hgqk", grouped, kv_block[0], preferred_element_type=jnp.float32) * head_dim ** -0.5
        offsets = key_block * block_len + jnp.arange(block_len)[None, :] - query_pos[:, None]
        allowed = offsets <= 0
        scores = jnp.where(allowed, scores, NEG_BIG)
        new_max = jnp.maximum(row_max, jnp.max(scores, axis=-1))
        weights = jnp.where(allowed, jnp.exp(scores - new_max[..., None]), 0.0)
        rescale = jnp.exp(row_max - new_max)
        row_sum = row_sum * rescale + jnp.sum(weights, axis=-1)
        acc_out = acc_out * rescale[..., None] + jnp.einsum("hgqk,khd->hgqd", weights.astype(jnp.bfloat16), kv_block[1], preferred_element_type=jnp.float32)
        return new_max, row_sum, acc_out

    stat_shape = (kv_heads, group_size, block_len)
    init_state = (
        jnp.full(stat_shape, NEG_BIG, jnp.float32),
        jnp.zeros(stat_shape, jnp.float32),
        jnp.zeros(stat_shape + (head_dim,), jnp.float32),
    )
    row_max, row_sum, acc_out = lax.fori_loop(zero_idx, block_id + 1, kv_step, init_state)
    attn_out = acc_out / row_sum[..., None]
    return jnp.transpose(attn_out, (2, 0, 1, 3)).reshape(block_len, num_heads, head_dim).astype(jnp.bfloat16)


def global_layer(hidden, dev_rank, num_dev, weights):
    w_query, w_key, w_value, w_out = weights
    queries, key_rows, value_rows = project_qkv(hidden, w_query, w_key, w_value)
    tok_rows, kv_heads, head_dim = key_rows.shape
    block_len = tok_rows // 2
    kv_all = lax.all_gather(jnp.stack([key_rows, value_rows]), "cp")
    kv_all = kv_all.reshape(num_dev, 2, 2, block_len, kv_heads, head_dim)
    lead_out = causal_block_attention(queries[:block_len], dev_rank, kv_all, num_dev)
    trail_out = causal_block_attention(queries[block_len:], 2 * num_dev - 1 - dev_rank, kv_all, num_dev)
    return residual_update(hidden, jnp.concatenate([lead_out, trail_out], axis=0), w_out)


def solution(mesh):
    num_dev = mesh.shape["cp"]

    def per_device(hidden, w_query, w_key, w_value, w_out):
        dev_rank = lax.axis_index("cp")
        num_layers = w_query.shape[0]
        for layer_idx in range(num_layers - 1):
            queries, key_rows, value_rows = project_qkv(hidden, w_query[layer_idx], w_key[layer_idx], w_value[layer_idx])
            halo_keys, halo_values = gather_halo(key_rows, value_rows, num_dev)
            attn_out = local_attention(queries, key_rows, value_rows, halo_keys, halo_values, dev_rank)
            hidden = residual_update(hidden, attn_out, w_out[layer_idx])
        hidden = to_output_layout(hidden, dev_rank, num_dev)
        last_layer = num_layers - 1
        last_weights = (w_query[last_layer], w_key[last_layer], w_value[last_layer], w_out[last_layer])
        return global_layer(hidden, dev_rank, num_dev, last_weights)

    row_spec = P(("dp", "cp"), None)
    return jax.shard_map(per_device, mesh=mesh, in_specs=(row_spec, P(), P(), P(), P()), out_specs=row_spec, check_vma=False)
```

profile of v0, /device:TPU:127, one launch (start us, length us, event | category | flops | bytes accessed | tf_op | source)
XLA Modules:
  0.0 1374.0 jit_solution(4892180955305384865)
XLA Ops:
  6.6 22.9 %fusion.424 = (bf16[1,2560,4,256]{3,2,1,0:T(4,128)(2,1)}, bf16[1,2560,4,256]{3,2,1,0:T(4,128)(2,1)}, bf16[1,2560,4,256]{3,2,1,0:T(4,128)(2,1)}, bf16[1,2560,4,25...) fusion(bf16[6,2560,4,256]{3,2,1,0:T(4,128)(2,1)} %param.11), kind=kLoop, calls=%fused_computation.509 | loop fusion | bytes 62914560 | tf_op jit(solution)/shard_map/slice | solution.py:159
  30.0 22.7 %fusion.425 = (bf16[1,2560,4,256]{3,2,1,0:T(4,128)(2,1)}, bf16[1,2560,4,256]{3,2,1,0:T(4,128)(2,1)}, bf16[1,2560,4,256]{3,2,1,0:T(4,128)(2,1)}, bf16[1,2560,4,25...) fusion(bf16[6,2560,4,256]{3,2,1,0:T(4,128)(2,1)} %param.12), kind=kLoop, calls=%fused_computation.510 | loop fusion | bytes 62914560 | tf_op jit(solution)/shard_map/slice | solution.py:153
  64.2 41.0 %fusion.423 = (bf16[1,2560,8,256]{3,2,1,0:T(8,128)(2,1)}, bf16[1,2560,8,256]{3,2,1,0:T(8,128)(2,1)}, bf16[1,2560,8,256]{3,2,1,0:T(8,128)(2,1)}, bf16[1,2560,8,25...) fusion(bf16[6,2560,8,256]{3,2,1,0:T(8,128)(2,1)} %param.10), kind=kLoop, calls=%fused_computation.508 | loop fusion | bytes 125829120 | tf_op jit(solution)/shard_map/slice | solution.py:159
  105.2 11.0 fusion.288
  148.5 9.5 fusion.143
  159.2 6.5 fusion.336
  178.4 46.0 %collective-permute-done.2 = bf16[2,512,4,256]{3,1,2,0:T(8,128)(2,1)S(1)} collective-permute-done((bf16[2,512,4,256]{3,1,2,0:T(8,128)(2,1)S(1)}, bf16[2,512,4,256]{3,1,2,0:T(8,128)(2,1)S(1)}, u32[]{:S(2)}, u32[]{:S(2)}) %collective-permute-start.2) | collective-permute-done | bytes 2097184 | tf_op jit(solution)/shard_map/ppermute | solution.py:54
  234.4 8.7 fusion.285
  251.2 9.4 fusion.142
  261.8 6.5 fusion.338
  280.3 61.0 %collective-permute-done.4 = bf16[2,512,4,256]{3,1,2,0:T(8,128)(2,1)S(1)} collective-permute-done((bf16[2,512,4,256]{3,1,2,0:T(8,128)(2,1)S(1)}, bf16[2,512,4,256]{3,1,2,0:T(8,128)(2,1)S(1)}, u32[]{:S(2)}, u32[]{:S(2)}) %collective-permute-start.4) | collective-permute-done | bytes 2097184 | tf_op jit(solution)/shard_map/ppermute | solution.py:54
  351.2 8.7 fusion.283
  362.0 6.0 fusion.282
  368.0 9.4 fusion.141
  378.6 6.5 fusion.340
  397.9 60.9 %collective-permute-done.6 = bf16[2,512,4,256]{3,1,2,0:T(8,128)(2,1)S(1)} collective-permute-done((bf16[2,512,4,256]{3,1,2,0:T(8,128)(2,1)S(1)}, bf16[2,512,4,256]{3,1,2,0:T(8,128)(2,1)S(1)}, u32[]{:S(2)}, u32[]{:S(2)}) %collective-permute-start.6) | collective-permute-done | bytes 2097184 | tf_op jit(solution)/shard_map/ppermute | solution.py:54
  468.6 8.7 fusion.281
  479.4 6.0 fusion.280
  485.4 9.4 fusion.140
  496.0 6.5 fusion.342
  515.1 61.0 %collective-permute-done.8 = bf16[2,512,4,256]{3,1,2,0:T(8,128)(2,1)S(1)} collective-permute-done((bf16[2,512,4,256]{3,1,2,0:T(8,128)(2,1)S(1)}, bf16[2,512,4,256]{3,1,2,0:T(8,128)(2,1)S(1)}, u32[]{:S(2)}, u32[]{:S(2)}) %collective-permute-start.8) | collective-permute-done | bytes 2097184 | tf_op jit(solution)/shard_map/ppermute | solution.py:54
  585.8 8.8 fusion.279
  602.7 9.7 fusion.139
  613.3 29.5 %collective-permute-start.10 = (bf16[256,2560]{1,0:T(8,128)(2,1)S(1)}, bf16[256,2560]{1,0:T(8,128)(2,1)}, u32[]{:S(2)}, u32[]{:S(2)}) collective-permute-start(bf16[256,2560]{1,0:T(8,128)(2,1)S(1)} %get-tuple-element.251), channel_id=1, source_target_pairs={{0,0},{1,2},{2,4},{3,6},{4,8},{5,10},{6,12},{7,14},{8,16},{9,18},{... | collective-permute-start | bytes 3932168 | tf_op jit(solution)/shard_map/ppermute | solution.py:88
  642.9 19.9 %collective-permute-done.10 = bf16[256,2560]{1,0:T(8,128)(2,1)} collective-permute-done((bf16[256,2560]{1,0:T(8,128)(2,1)S(1)}, bf16[256,2560]{1,0:T(8,128)(2,1)}, u32[]{:S(2)}, u32[]{:S(2)}) %collective-permute-start.10) | collective-permute-done | bytes 1310752 | tf_op jit(solution)/shard_map/ppermute | solution.py:88
  662.9 11.3 collective-permute-done.11
  687.1 8.6 fusion.293
  696.8 190.2 %all-gather.3.cloned.1.call-done = bf16[64,512,4,256]{3,1,2,0:T(8,128)(2,1)} async-done(((bf16[2,512,4,256]{3,1,2,0:T(8,128)(2,1)}), bf16[64,512,4,256]{3,1,2,0:T(8,128)(2,1)}) %all-gather.3.cloned.1.call-update) | async-done | bytes 67108880 | tf_op jit(solution)/shard_map/all_gather | solution.py:139
  887.0 44.2 %copy.68 = bf16[32,2,2,256,4,256]{5,3,4,2,1,0:T(8,128)(2,1)} copy(bf16[32,2,2,256,4,256]{5,3,2,4,1,0:T(8,128)(2,1)} %bitcast.145) | data formatting | bytes 134217728
  932.7 212.7 %while.30 = (s32[]{:T(128)}, f32[4,2,256]{2,1,0:T(2,128)S(1)}, f32[4,2,256]{2,1,0:T(2,128)S(1)}, f32[4,2,256,256]{3,2,1,0:T(8,128)}, s32[]{:T(128)}, /*index=5*/...) while((s32[]{:T(128)}, f32[4,2,256]{2,1,0:T(2,128)S(1)}, ...), condition=%wide.region_34.35_spmd.clone, body=%wide.region_31.34_spmd.clone.sunk | while | flops 544870912 | bytes 12980490 | solution.py:129
  1146.9 206.6 %while.31 = (s32[]{:T(128)}, f32[4,2,256]{2,1,0:T(2,128)S(1)}, f32[4,2,256]{2,1,0:T(2,128)S(1)}, f32[4,2,256,256]{3,2,1,0:T(8,128)}, s32[]{:T(128)}, /*index=5*/...) while((s32[]{:T(128)}, f32[4,2,256]{2,1,0:T(2,128)S(1)}, ...), condition=%wide.region_38.39_spmd.clone, body=%wide.region_35.38_spmd.clone.sunk | while | flops 544870912 | bytes 12980490 | solution.py:129
  1356.1 8.7 fusion.138
  (755 shorter events, 597.6 us)
Async XLA Ops:
  6.5 22.9 %copy-start.9 = (bf16[512,2560]{1,0:T(8,128)(2,1)S(1)}, bf16[512,2560]{1,0:T(8,128)(2,1)}, u32[]{:S(2)}) copy-start(bf16[512,2560]{1,0:T(8,128)(2,1)} %param.9) | copy-start | bytes 7864324
  6.5 880.4 %all-gather.3.cloned.1.call-start = ((), (), s32[]{:S(2)}) async-start(), calls=%async_computation | async-start | bytes 69206016 | tf_op jit(solution)/shard_map/all_gather | solution.py:139
  61.1 59.8 %collective-permute-start = (bf16[2,512,4,256]{3,1,2,0:T(8,128)(2,1)}, bf16[2,512,4,256]{3,1,2,0:T(8,128)(2,1)}, u32[]{:S(2)}, u32[]{:S(2)}) collective-permute-start(bf16[2,512,4,256]{3,1,2,0:T(8,128)(2,1)} %pad_maximum_fusion.11), channel_id=1, source_target_pairs={{0,2},{1,3},{2,4},{3,5},{4,6},{5,7},{6,8},{7,9},{8,10},{9,11},{10,... | collective-permute-start | bytes 6291464 | tf_op jit(solution)/shard_map/ppermute | solution.py:54
  62.4 60.2 %collective-permute-start.1 = (bf16[2,512,4,256]{3,1,2,0:T(8,128)(2,1)}, bf16[2,512,4,256]{3,1,2,0:T(8,128)(2,1)}, u32[]{:S(2)}, u32[]{:S(2)}) collective-permute-start(bf16[2,512,4,256]{3,1,2,0:T(8,128)(2,1)} %pad_maximum_fusion.11), channel_id=1, source_target_pairs={{0,1},{1,2},{2,3},{3,4},{4,5},{5,6},{6,7},{7,8},{8,9},{9,10},{10,1... | collective-permute-start | bytes 6291464 | tf_op jit(solution)/shard_map/ppermute | solution.py:54
  148.5 9.5 copy-start.10
  159.1 13.2 copy-start.17
  165.7 60.7 %copy-start.27 = (bf16[512,4,256]{2,0,1:T(8,128)(2,1)}, bf16[512,4,256]{2,0,1:T(8,128)(2,1)S(1)}, u32[]{:S(2)}) copy-start(bf16[512,4,256]{2,0,1:T(8,128)(2,1)S(1)} %fusion.336) | copy-start | bytes 3145732
  169.7 54.7 %collective-permute-start.2 = (bf16[2,512,4,256]{3,1,2,0:T(8,128)(2,1)S(1)}, bf16[2,512,4,256]{3,1,2,0:T(8,128)(2,1)S(1)}, u32[]{:S(2)}, u32[]{:S(2)}) collective-permute-start(bf16[2,512,4,256]{3,1,2,0:T(8,128)(2,1)S(1)} %pad_maximum_fusion.12), channel_id=1, source_target_pairs={{0,2},{1,3},{2,4},{3,5},{4,6},{5,7},{6,8},{7,9},{8,10},{9,11},{10,... | collective-permute-start | bytes 6291464 | tf_op jit(solution)/shard_map/ppermute | solution.py:54
  171.0 53.6 %collective-permute-start.3 = (bf16[2,512,4,256]{3,1,2,0:T(8,128)(2,1)S(1)}, bf16[2,512,4,256]{3,1,2,0:T(8,128)(2,1)S(1)}, u32[]{:S(2)}, u32[]{:S(2)}) collective-permute-start(bf16[2,512,4,256]{3,1,2,0:T(8,128)(2,1)S(1)} %pad_maximum_fusion.12), channel_id=1, source_target_pairs={{0,1},{1,2},{2,3},{3,4},{4,5},{5,6},{6,7},{7,8},{8,9},{9,10},{10,1... | collective-permute-start | bytes 6291464 | tf_op jit(solution)/shard_map/ppermute | solution.py:54
  251.2 9.5 copy-start.18
  261.7 12.5 copy-start.11
  268.3 75.0 %copy-start.28 = (bf16[512,4,256]{2,0,1:T(8,128)(2,1)}, bf16[512,4,256]{2,0,1:T(8,128)(2,1)S(1)}, u32[]{:S(2)}) copy-start(bf16[512,4,256]{2,0,1:T(8,128)(2,1)S(1)} %fusion.338) | copy-start | bytes 3145732
  271.5 69.9 %collective-permute-start.4 = (bf16[2,512,4,256]{3,1,2,0:T(8,128)(2,1)S(1)}, bf16[2,512,4,256]{3,1,2,0:T(8,128)(2,1)S(1)}, u32[]{:S(2)}, u32[]{:S(2)}) collective-permute-start(bf16[2,512,4,256]{3,1,2,0:T(8,128)(2,1)S(1)} %pad_maximum_fusion.13), channel_id=1, source_target_pairs={{0,2},{1,3},{2,4},{3,5},{4,6},{5,7},{6,8},{7,9},{8,10},{9,11},{10,... | collective-permute-start | bytes 6291464 | tf_op jit(solution)/shard_map/ppermute | solution.py:54
  272.9 68.6 %collective-permute-start.5 = (bf16[2,512,4,256]{3,1,2,0:T(8,128)(2,1)S(1)}, bf16[2,512,4,256]{3,1,2,0:T(8,128)(2,1)S(1)}, u32[]{:S(2)}, u32[]{:S(2)}) collective-permute-start(bf16[2,512,4,256]{3,1,2,0:T(8,128)(2,1)S(1)} %pad_maximum_fusion.13), channel_id=1, source_target_pairs={{0,1},{1,2},{2,3},{3,4},{4,5},{5,6},{6,7},{7,8},{8,9},{9,10},{10,1... | collective-permute-start | bytes 6291464 | tf_op jit(solution)/shard_map/ppermute | solution.py:54
  368.0 9.5 copy-start.12
  378.6 13.1 copy-start.13
  385.1 75.5 %copy-start.29 = (bf16[512,4,256]{2,0,1:T(8,128)(2,1)}, bf16[512,4,256]{2,0,1:T(8,128)(2,1)S(1)}, u32[]{:S(2)}) copy-start(bf16[512,4,256]{2,0,1:T(8,128)(2,1)S(1)} %fusion.340) | copy-start | bytes 3145732
  389.1 69.6 %collective-permute-start.6 = (bf16[2,512,4,256]{3,1,2,0:T(8,128)(2,1)S(1)}, bf16[2,512,4,256]{3,1,2,0:T(8,128)(2,1)S(1)}, u32[]{:S(2)}, u32[]{:S(2)}) collective-permute-start(bf16[2,512,4,256]{3,1,2,0:T(8,128)(2,1)S(1)} %pad_maximum_fusion.14), channel_id=1, source_target_pairs={{0,2},{1,3},{2,4},{3,5},{4,6},{5,7},{6,8},{7,9},{8,10},{9,11},{10,... | collective-permute-start | bytes 6291464 | tf_op jit(solution)/shard_map/ppermute | solution.py:54
  390.4 68.4 %collective-permute-start.7 = (bf16[2,512,4,256]{3,1,2,0:T(8,128)(2,1)S(1)}, bf16[2,512,4,256]{3,1,2,0:T(8,128)(2,1)S(1)}, u32[]{:S(2)}, u32[]{:S(2)}) collective-permute-start(bf16[2,512,4,256]{3,1,2,0:T(8,128)(2,1)S(1)} %pad_maximum_fusion.14), channel_id=1, source_target_pairs={{0,1},{1,2},{2,3},{3,4},{4,5},{5,6},{6,7},{7,8},{8,9},{9,10},{10,1... | collective-permute-start | bytes 6291464 | tf_op jit(solution)/shard_map/ppermute | solution.py:54
  485.4 9.5 copy-start.14
  495.9 13.1 copy-start.15
  502.5 75.6 %copy-start.30 = (bf16[512,4,256]{2,0,1:T(8,128)(2,1)}, bf16[512,4,256]{2,0,1:T(8,128)(2,1)S(1)}, u32[]{:S(2)}) copy-start(bf16[512,4,256]{2,0,1:T(8,128)(2,1)S(1)} %fusion.342) | copy-start | bytes 3145732
  506.4 69.7 %collective-permute-start.8 = (bf16[2,512,4,256]{3,1,2,0:T(8,128)(2,1)S(1)}, bf16[2,512,4,256]{3,1,2,0:T(8,128)(2,1)S(1)}, u32[]{:S(2)}, u32[]{:S(2)}) collective-permute-start(bf16[2,512,4,256]{3,1,2,0:T(8,128)(2,1)S(1)} %pad_maximum_fusion.15), channel_id=1, source_target_pairs={{0,2},{1,3},{2,4},{3,5},{4,6},{5,7},{6,8},{7,9},{8,10},{9,11},{10,... | collective-permute-start | bytes 6291464 | tf_op jit(solution)/shard_map/ppermute | solution.py:54
  507.7 68.5 %collective-permute-start.9 = (bf16[2,512,4,256]{3,1,2,0:T(8,128)(2,1)S(1)}, bf16[2,512,4,256]{3,1,2,0:T(8,128)(2,1)S(1)}, u32[]{:S(2)}, u32[]{:S(2)}) collective-permute-start(bf16[2,512,4,256]{3,1,2,0:T(8,128)(2,1)S(1)} %pad_maximum_fusion.15), channel_id=1, source_target_pairs={{0,1},{1,2},{2,3},{3,4},{4,5},{5,6},{6,7},{7,8},{8,9},{9,10},{10,1... | collective-permute-start | bytes 6291464 | tf_op jit(solution)/shard_map/ppermute | solution.py:54
  602.7 9.7 copy-start.16
  613.3 49.5 %collective-permute-start.10 = (bf16[256,2560]{1,0:T(8,128)(2,1)S(1)}, bf16[256,2560]{1,0:T(8,128)(2,1)}, u32[]{:S(2)}, u32[]{:S(2)}) collective-permute-start(bf16[256,2560]{1,0:T(8,128)(2,1)S(1)} %get-tuple-element.251), channel_id=1, source_target_pairs={{0,0},{1,2},{2,4},{3,6},{4,8},{5,10},{6,12},{7,14},{8,16},{9,18},{... | collective-permute-start | bytes 3932168 | tf_op jit(solution)/shard_map/ppermute | solution.py:88
  642.8 31.4 %collective-permute-start.11 = (bf16[256,2560]{1,0:T(8,128)(2,1)S(1)}, bf16[256,2560]{1,0:T(8,128)(2,1)}, u32[]{:S(2)}, u32[]{:S(2)}) collective-permute-start(bf16[256,2560]{1,0:T(8,128)(2,1)S(1)} %get-tuple-element.252), channel_id=1, source_target_pairs={{0,1},{1,3},{2,5},{3,7},{4,9},{5,11},{6,13},{7,15},{8,17},{9,19},{... | collective-permute-start | bytes 3932168 | tf_op jit(solution)/shard_map/ppermute | solution.py:89
  674.2 8.4 slice-start.12
  676.2 10.8 copy-start.1
  676.2 10.8 copy-start.3
  1356.1 8.7 copy-start.2
  1356.1 8.7 copy-start.4
  (34 other events, 171.3 us)
Sparse Core Ops, SparseCore 0:
  687.2 199.7 all-gather.2
where the time goes:
time: 1390 us; the launch traced here: 1370 us
  matrix products  626 us (45%)
  waiting for transfers between devices  450 us (32%)
  local copies, waits for them, and re-layouts  155 us (11%)
  other arithmetic  82.5 us (6%)
  starting transfers between devices  43.2 us (3%)
  between operations  15.1 us (1%)
    dot_general x65, matrix products, kv_step(): jnp.einsum('hgqk,khd->hgqd', weights.astype(jnp.bfloat16), kv_block[1], p...  263 us
    ppermute x10, waiting for transfers between devices, gather_halo(): pieces.append(lax.ppermute(tail_kv, 'cp', perm_pairs))  229 us
    all_gather x1, waiting for transfers between devices, global_layer(): kv_all = lax.all_gather(jnp.stack([key_rows, value_rows]), 'cp')  190 us
    dot_general x65, matrix products, kv_step(): jnp.einsum('qhgd,khd->hgqk', grouped, kv_block[0], preferred_element_type...  112 us
    dot_general x10, matrix products, window_attention(): jnp.einsum('hgqk,khd->hgqd', weights.astype(jnp.bfloat16), value_rows, pr...  70.4 us
    dot_general x6, matrix products, residual_update(): jnp.einsum('the,hed->td', attn_out, w_out, preferred_element_type=jnp.flo...  56.2 us
    unnamed x112, local copies, waits for them, and re-layouts  50.2 us
    dot_general x6, matrix products, project_qkv(): jnp.einsum('td,dhe->the', normed, w_query, preferred_element_type=jnp.flo...  43.1 us
  transfers between devices with their start and end apart: 13, of which 7 were waited for; matrix products, arithmetic and copies ran while one was open for 7% of the time, Pallas kernels for 0%

commit v1 on v0

v1 whole, which is shorter than its diff:
```python
import functools

import jax
import jax.numpy as jnp
import numpy as np
from jax import lax
from jax.experimental import pallas as pl
from jax.experimental.pallas import tpu as pltpu
from jax.sharding import PartitionSpec as P

WINDOW = 1024
EPS_NORM = 1e-6
NEG_BIG = -1e30
LOG2E = 1.4426950408889634
MESH = pl.DeviceIdType.MESH
NT = (((1,), (1,)), ((), ()))


def rms_normed(rows_in):
    widened = rows_in.astype(jnp.float32)
    return widened * lax.rsqrt(jnp.mean(widened * widened, axis=-1, keepdims=True) + EPS_NORM)


def iota2(shape, dim):
    return lax.broadcasted_iota(jnp.int32, shape, dim)


def perm_matrix(heads):
    dn = 128 // heads
    row = np.arange(256)
    h, ct, d = row // (2 * dn), (row // dn) % 2, row % dn
    out = np.zeros((256, 256), np.float32)
    out[row, d * 2 * heads + ct * heads + h] = 1
    return jnp.asarray(out, jnp.bfloat16)


def relayout_kernel(heads, perm, w_in, w_out):
    dn = 128 // heads
    for b in range(w_in.shape[1] // 512):
        pair = jnp.concatenate([w_in[0, b * 512:b * 512 + 256, :], w_in[0, b * 512 + 256:b * 512 + 512, :]], axis=1)
        moved = jnp.dot(perm[...], pair, preferred_element_type=jnp.float32).astype(jnp.bfloat16)
        for h in range(heads):
            for ct in range(2):
                row, col = (h * 2 + ct) * dn, h * 256 + ct * 128
                for i in range(2):
                    d0 = (2 * b + i) * dn
                    w_out[0, d0:d0 + dn, col:col + 128] = moved[row:row + dn, i * 128:(i + 1) * 128]


def flat_heads(w):
    layers, width, heads, head = w.shape
    rows = w.reshape(layers, width, heads, 2, 128).transpose(0, 1, 3, 2, 4).reshape(layers, width * 2 * heads, 128)
    step = 512
    return pl.pallas_call(
        functools.partial(relayout_kernel, heads),
        grid=(layers, width // step),
        in_specs=[pl.BlockSpec((256, 256), lambda l, i: (0, 0)), pl.BlockSpec((1, step * 2 * heads, 128), lambda l, i: (l, i, 0))],
        out_specs=pl.BlockSpec((1, step, heads * head), lambda l, i: (l, i, 0)),
        out_shape=jax.ShapeDtypeStruct((layers, width, heads * head), w.dtype),
        name="flat_heads",
    )(perm_matrix(heads), rows)


def local_kernel(num_dev, num_layers, x_in, wq_hbm, wk_hbm, wv_hbm, wo_hbm, x_out,
                 n_s, q_s, own_s, halo_a, halo_b, o_s, acc, wkv_buf, wq_buf, wo_buf,
                 kv_sem, q_sem, o_sem, send_a, send_b, recv_a, recv_b, credit_a, credit_b):
    me = lax.axis_index("cp")
    odd = lax.rem(me, 2) == 1
    partner = jnp.where(odd, me - 1, me + 1)
    fwd = lax.rem(me + 2, num_dev)
    back = lax.rem(me + num_dev - 2, num_dev)
    rows, width = n_s.shape
    half = rows // 2
    kv_heads = own_s.shape[0]
    head = own_s.shape[-1]
    scale = head ** -0.5 * LOG2E
    chunk = 32

    barrier = pltpu.get_barrier_semaphore()
    for other in (fwd, back, partner):
        pl.semaphore_signal(barrier, inc=1, device_id={"cp": other}, device_id_type=MESH)
    pl.semaphore_wait(barrier, 3)

    def kv_copies(layer, h):
        slot = lax.rem(h, 2)
        cols = pl.ds(pl.multiple_of(h * head, head), head)
        return (pltpu.make_async_copy(wk_hbm.at[layer, :, cols], wkv_buf.at[slot, 0], kv_sem.at[slot, 0]),
                pltpu.make_async_copy(wv_hbm.at[layer, :, cols], wkv_buf.at[slot, 1], kv_sem.at[slot, 1]))

    def q_copy(layer, h):
        slot = lax.rem(h, 2)
        cols = pl.ds(pl.multiple_of(h * 2 * head, 2 * head), 2 * head)
        return pltpu.make_async_copy(wq_hbm.at[layer, :, cols], wq_buf.at[slot], q_sem.at[slot])

    def o_copy(layer, h):
        slot = lax.rem(h, 2)
        part = pl.ds(pl.multiple_of(h * 2 * head, 2 * head), 2 * head)
        return pltpu.make_async_copy(wo_hbm.at[layer, part], wo_buf.at[slot], o_sem.at[slot])

    def start_kv(layer, h):
        for copy in kv_copies(layer, h):
            copy.start()

    def prefetch(start, layer, h):
        @pl.when(h < kv_heads - 2)
        def _():
            start(layer, h + 2)

        @pl.when(jnp.logical_and(h >= kv_heads - 2, layer < num_layers - 1))
        def _():
            start(layer + 1, h + 2 - kv_heads)

    for h in range(2):
        start_kv(0, h)
        q_copy(0, h).start()
        o_copy(0, h).start()

    def send_own(parity, h):
        return pltpu.make_async_remote_copy(
            src_ref=own_s.at[h], dst_ref=halo_a.at[parity, h], send_sem=send_a.at[h], recv_sem=recv_a.at[parity, h],
            device_id={"cp": fwd}, device_id_type=MESH)

    def send_partner(parity, h, src):
        return pltpu.make_async_remote_copy(
            src_ref=src, dst_ref=halo_b.at[parity, h], send_sem=send_b.at[h], recv_sem=recv_b.at[parity, h],
            device_id={"cp": partner}, device_id_type=MESH)

    def norm_rows(i, carry):
        part = pl.ds(pl.multiple_of(i * chunk, chunk), chunk)
        n_s[part, :] = rms_normed(x_in[part, :]).astype(jnp.bfloat16)
        x_out[part, :] = x_in[part, :]
        return carry

    lax.fori_loop(0, rows // chunk, norm_rows, 0)

    bias_a = jnp.where(me < 2, NEG_BIG, 0.0)
    bias_b = jnp.where(me < 1, NEG_BIG, 0.0)

    def attend(parity, h, j):
        blocks = [(halo_a.at[parity, h], 0, bias_a), (halo_a.at[parity, h], 1, bias_a),
                  (halo_b.at[parity, h], 0, bias_b), (halo_b.at[parity, h], 1, bias_b),
                  (own_s.at[h], 0, None), (own_s.at[h], 1, None)][j:j + 5]
        q_tile = q_s[h, j]
        row = lax.rem(iota2((2 * half, half), 0), half)
        key = iota2((2 * half, half), 1)
        tiles = []
        for i, (ref, part, bias) in enumerate(blocks):
            keys = ref[0, part * half:(part + 1) * half, :]
            scores = lax.dot_general(q_tile, keys, NT, preferred_element_type=jnp.float32) * scale
            if bias is not None:
                scores = scores + bias
            if i == 0:
                scores = jnp.where(key > row, scores, NEG_BIG)
            if i == len(blocks) - 1:
                scores = jnp.where(key <= row, scores, NEG_BIG)
            tiles.append(scores)
        top = jnp.max(functools.reduce(jnp.maximum, tiles), axis=-1, keepdims=True)
        total, out = None, None
        for scores, (ref, part, _) in zip(tiles, blocks):
            e = jnp.exp2(scores - top)
            total = e if total is None else total + e
            term = jnp.dot(e.astype(jnp.bfloat16), ref[1, part * half:(part + 1) * half, :], preferred_element_type=jnp.float32)
            out = term if out is None else out + term
        out = (out / jnp.sum(total, axis=-1, keepdims=True)).astype(jnp.bfloat16)
        for g in range(2):
            o_s[j * half:(j + 1) * half, g * head:(g + 1) * head] = out[g * half:(g + 1) * half, :]

    def layer_step(layer, carry):
        parity = lax.rem(layer, 2)

        @pl.when(layer >= 2)
        def _():
            pl.semaphore_wait(credit_a, 1)
            pl.semaphore_wait(credit_b, 1)

        def kv_step(h, c):
            slot = lax.rem(h, 2)
            for copy in kv_copies(layer, h):
                copy.wait()
            for i in range(2):
                own_s[h, i] = jnp.dot(n_s[...], wkv_buf[slot, i], preferred_element_type=jnp.float32).astype(jnp.bfloat16)
            prefetch(start_kv, layer, h)
            send_own(parity, h).start()

            @pl.when(jnp.logical_not(odd))
            def _():
                send_partner(parity, h, own_s.at[h]).start()
            return c

        lax.fori_loop(0, kv_heads, kv_step, 0)

        def q_step(h, c):
            slot = lax.rem(h, 2)
            q_copy(layer, h).wait()
            for g in range(2):
                q = jnp.dot(n_s[...], wq_buf[slot, :, g * head:(g + 1) * head], preferred_element_type=jnp.float32).astype(jnp.bfloat16)
                for j in range(2):
                    q_s[h, j, g * half:(g + 1) * half, :] = q[j * half:(j + 1) * half, :]
            prefetch(lambda *a: q_copy(*a).start(), layer, h)
            return c

        lax.fori_loop(0, kv_heads, q_step, 0)

        def attn_step(h, c):
            slot = lax.rem(h, 2)
            send_own(parity, h).wait_recv()

            @pl.when(odd)
            def _():
                send_partner(parity, h, halo_a.at[parity, h]).start()
            send_partner(parity, h, own_s.at[h]).wait_recv()
            attend(parity, h, 0)
            attend(parity, h, 1)
            o_copy(layer, h).wait()

            def out_part(i, cc):
                cols = pl.ds(pl.multiple_of(i * 512, 512), 512)
                part = jnp.dot(o_s[...], wo_buf[slot, :, cols], preferred_element_type=jnp.float32)

                @pl.when(h == 0)
                def _():
                    acc[:, cols] = part

                @pl.when(h > 0)
                def _():
                    acc[:, cols] = acc[:, cols] + part
                return cc

            lax.fori_loop(0, width // 512, out_part, 0)
            prefetch(lambda *a: o_copy(*a).start(), layer, h)
            return c

        lax.fori_loop(0, kv_heads, attn_step, 0)

        def drain(h, c):
            send_own(parity, h).wait_send()
            send_partner(parity, h, own_s.at[h]).wait_send()
            return c

        lax.fori_loop(0, kv_heads, drain, 0)

        @pl.when(layer < num_layers - 2)
        def _():
            pl.semaphore_signal(credit_a, inc=1, device_id={"cp": back}, device_id_type=MESH)
            pl.semaphore_signal(credit_b, inc=1, device_id={"cp": partner}, device_id_type=MESH)

        def update_rows(i, c):
            part = pl.ds(pl.multiple_of(i * 16, 16), 16)
            new = (x_out[part, :].astype(jnp.float32) + rms_normed(acc[part, :])).astype(jnp.bfloat16)
            x_out[part, :] = new
            n_s[part, :] = rms_normed(new).astype(jnp.bfloat16)
            return c

        lax.fori_loop(0, rows // 16, update_rows, 0)
        return carry

    lax.fori_loop(0, num_layers, layer_step, 0)


def local_layers(hidden, w_query, w_key, w_value, w_out, num_dev, num_layers):
    rows, width = hidden.shape
    kv_width = w_key.shape[2]
    head = 256
    kv_heads = kv_width // head
    half = rows // 2
    bf16, f32 = jnp.bfloat16, jnp.float32
    hbm = pl.BlockSpec(memory_space=pltpu.HBM)
    vmem = pl.BlockSpec(memory_space=pltpu.VMEM)
    dma = pltpu.SemaphoreType.DMA
    return pl.pallas_call(
        functools.partial(local_kernel, num_dev, num_layers),
        out_shape=jax.ShapeDtypeStruct((rows, width), bf16),
        in_specs=[vmem, hbm, hbm, hbm, hbm],
        out_specs=vmem,
        scratch_shapes=[
            pltpu.VMEM((rows, width), bf16),
            pltpu.VMEM((kv_heads, 2, 2 * half, head), bf16),
            pltpu.VMEM((kv_heads, 2, rows, head), bf16),
            pltpu.VMEM((2, kv_heads, 2, rows, head), bf16),
            pltpu.VMEM((2, kv_heads, 2, rows, head), bf16),
            pltpu.VMEM((rows, 2 * head), bf16),
            pltpu.VMEM((rows, width), f32),
            pltpu.VMEM((2, 2, width, head), bf16),
            pltpu.VMEM((2, width, 2 * head), bf16),
            pltpu.VMEM((2, 2 * head, width), bf16),
            dma((2, 2)), dma((2,)), dma((2,)),
            dma((kv_heads,)), dma((kv_heads,)), dma((2, kv_heads)), dma((2, kv_heads)),
            pltpu.SemaphoreType.REGULAR, pltpu.SemaphoreType.REGULAR,
        ],
        compiler_params=pltpu.CompilerParams(collective_id=0, has_side_effects=True, vmem_limit_bytes=62 * 1024 * 1024),
        name="local_layers",
    )(hidden, w_query, w_key, w_value, w_out)


def flash_kernel(num_dev, q_ref, kv_hbm, out_ref, kv_buf, acc, m_s, l_s, sems):
    me = lax.axis_index("cp")
    half = q_ref.shape[1] // 2
    head = q_ref.shape[2]
    scale = head ** -0.5 * LOG2E
    num_rows = q_ref.shape[1]
    step_keys = kv_buf.shape[2]
    blocks = (me, 2 * num_dev - 1 - me)
    need = [(b * half + half + step_keys - 1) // step_keys for b in blocks]
    copies=lambda c: pltpu.make_async_copy(kv_hbm.at[c], kv_buf.at[c], sems.at[c])
    def start(c, carry):
        copies(c).start(); return carry
    lax.fori_loop(0, need[1], start, 0)
    m_s[...] = jnp.full(m_s.shape, NEG_BIG, jnp.float32)
    l_s[...] = jnp.zeros(l_s.shape, jnp.float32)
    acc[...] = jnp.zeros(acc.shape, jnp.float32)
    def one_tile(c, b, masked):
        s = lax.dot_general(q_ref[b], kv_buf[c, 0], NT, preferred_element_type=jnp.float32) * scale
        if masked:
            row = blocks[b] * half + lax.rem(iota2((num_rows, step_keys), 0), half)
            key = c * step_keys + iota2((num_rows, step_keys), 1)
            s = jnp.where(key <= row, s, NEG_BIG)
        old = m_s[b]
        top = jnp.maximum(old, jnp.max(s, axis=-1, keepdims=True))
        e = jnp.exp2(s - jnp.concatenate([top] * (step_keys // 128), axis=1))
        fix = jnp.exp2(old - top)
        m_s[b] = top
        part = e[:, 0:128]
        for i in range(1, step_keys // 128):
            part = part + e[:, i * 128:(i + 1) * 128]
        l_s[b] = l_s[b] * fix + part
        acc[b] = acc[b] * jnp.concatenate([fix] * (head // 128), axis=1) + jnp.dot(e.astype(jnp.bfloat16), kv_buf[c, 1], preferred_element_type=jnp.float32)
    def tile(c, b):
        edge = c == need[b] - 1
        @pl.when(edge)
        def _(): one_tile(c, b, True)
        @pl.when(jnp.logical_not(edge))
        def _(): one_tile(c, b, False)
    def body(c, carry):
        copies(c).wait()
        tile(c, 1)
        @pl.when(c < need[0])
        def _(): tile(c, 0)
        return carry
    lax.fori_loop(0, need[1], body, 0)
    for b in range(2):
        inv = 1.0 / jnp.sum(l_s[b],axis=-1,keepdims=True)
        out = (acc[b] * inv).astype(jnp.bfloat16)
        for g in range(2):
            out_ref[b * half:(b + 1) * half, g * head:(g + 1) * head] = out[g * half:(g + 1) * half]
def flash_head(queries, kv_all, num_dev):
    _, num_rows, head = queries.shape
    half = num_rows // 2
    f32 = jnp.float32
    nch=kv_all.shape[0]; tok = kv_all.shape[2]
    return pl.pallas_call(
        functools.partial(flash_kernel, num_dev),
        out_shape=jax.ShapeDtypeStruct((2 * half, 2 * head), jnp.bfloat16),
        in_specs=[pl.BlockSpec(memory_space=pltpu.VMEM), pl.BlockSpec(memory_space=pltpu.HBM)],
        out_specs=pl.BlockSpec(memory_space=pltpu.VMEM),
        scratch_shapes=[pltpu.VMEM((nch, 2, tok, head), jnp.bfloat16), pltpu.VMEM((2, num_rows, head), f32),
            pltpu.VMEM((2, num_rows, 128), f32), pltpu.VMEM((2, num_rows, 128), f32), pltpu.SemaphoreType.DMA((nch,))],
        compiler_params=pltpu.CompilerParams(vmem_limit_bytes=48 * 1024 * 1024),
        cost_estimate=pl.CostEstimate(flops=20_000_000_000, bytes_accessed=16_000_000, transcendentals=0), name="flash_head")(queries, kv_all)


def output_owner(block_idx, num_dev):
    return block_idx if block_idx < num_dev else 2 * num_dev - 1 - block_idx


def to_output_layout(hidden, dev_rank, num_dev):
    block_len = hidden.shape[0] // 2
    even_pairs = [(source, output_owner(2 * source, num_dev)) for source in range(num_dev)]
    odd_pairs = [(source, output_owner(2 * source + 1, num_dev)) for source in range(num_dev)]
    from_even = lax.ppermute(hidden[:block_len], "cp", even_pairs)
    from_odd = lax.ppermute(hidden[block_len:], "cp", odd_pairs)
    is_even = dev_rank % 2 == 0
    lead_rows = jnp.where(is_even, from_even, from_odd)
    trail_rows = jnp.where(is_even, from_odd, from_even)
    return jnp.concatenate([lead_rows, trail_rows], axis=0)


def solution(mesh):
    num_dev = mesh.shape["cp"]

    def per_device(hidden, w_query, w_key, w_value, w_out):
        dev_rank = lax.axis_index("cp")
        layers, width, heads, head = w_query.shape
        kv_heads = w_key.shape[2]
        group = heads // kv_heads
        wq = flat_heads(w_query)
        wk = flat_heads(w_key)
        wv = flat_heads(w_value)
        wo = w_out.reshape(layers, heads * head, width)
        last = layers - 1
        hidden = local_layers(hidden, wq, wk, wv, wo, num_dev, last)
        rows = hidden.shape[0]
        half = rows // 2
        normed = rms_normed(hidden).astype(jnp.bfloat16)
        gathered = []
        for h in range(kv_heads):
            cols = slice(h * head, (h + 1) * head)
            k = jnp.dot(normed, wk[last][:, cols], preferred_element_type=jnp.float32).astype(jnp.bfloat16)
            v = jnp.dot(normed, wv[last][:, cols], preferred_element_type=jnp.float32).astype(jnp.bfloat16)
            gathered.append(lax.all_gather(jnp.stack([k, v]), "cp"))
        hidden = to_output_layout(hidden, dev_rank, num_dev)
        normed = rms_normed(hidden).astype(jnp.bfloat16)
        queries = jnp.dot(normed, wq[last], preferred_element_type=jnp.float32).astype(jnp.bfloat16)
        queries = queries.reshape(2, half, kv_heads, group, head)
        outs = []
        for h in range(kv_heads):
            q = jnp.transpose(queries[:, :, h], (0, 2, 1, 3)).reshape(2, group * half, head)
            outs.append(flash_head(q, gathered[h], num_dev))
        attn = jnp.concatenate(outs, axis=1)
        update = jnp.dot(attn, wo[last], preferred_element_type=jnp.float32)
        return (hidden.astype(jnp.float32) + rms_normed(update)).astype(jnp.bfloat16)

    row_spec = P(("dp", "cp"), None)
    return jax.shard_map(per_device, mesh=mesh, in_specs=(row_spec, P(), P(), P(), P()), out_specs=row_spec, check_vma=False)
```

time: 1390 us -> 829 us (0.60)
  matrix products: 626 us -> 36.6 us
  Pallas kernels: 0 us -> 552 us
  waiting for transfers between devices: 450 us -> 164 us
  local copies, waits for them, and re-layouts: 155 us -> 27 us
  other arithmetic: 82.5 us -> 8.71 us
  starting transfers between devices: 43.2 us -> 11.7 us
    dot_general x174 -> x10, matrix products: 626 us -> 36.6 us  [the longest x4 9.74 us: per_device(): jnp.dot(normed, wk[last][:, cols], preferred_element_type=jnp.float32)]
    pallas_call x0 -> x8, Pallas kernels: none -> 552 us  [the longest x1 299 us: local_layers(): pl.pallas_call(functools.partial(local_kernel, num_dev, num_layers), out_...]
    ppermute x10 -> x0, waiting for transfers between devices: 229 us -> none  [gather_halo(): pieces.append(lax.ppermute(tail_kv, 'cp', perm_pairs))]
    slice x9 -> x2, local copies, waits for them, and re-layouts: 91.1 us -> 10.1 us  [the longest x1 8.56 us: per_device(): update = jnp.dot(attn, wo[last], preferred_element_type=jnp.float32)]
    reduce_sum x75 -> x0, other arithmetic: 55.3 us -> none  [the longest x65 33.8 us: kv_step(): row_sum = row_sum * rescale + jnp.sum(weights, axis=-1)]
    unnamed x112 -> x14, local copies, waits for them, and re-layouts: 50.2 us -> 1.22 us
    all_gather x1 -> x4, waiting for transfers between devices: 190 us -> 146 us  [per_device(): gathered.append(lax.all_gather(jnp.stack([k, v]), 'cp'))]
    ppermute x1, starting transfers between devices: 29.5 us -> 6.97 us  [to_output_layout(): from_even = lax.ppermute(hidden[:block_len], 'cp', even_pairs)]
  transfers between devices with their start and end apart: 13 -> 6, of which waited for: 7 -> 6; matrix products, arithmetic and copies ran while one was open for 7% -> 5% of each run, Pallas kernels for 0% -> 11%
where the time goes in v1:
time: 829 us; the launch traced here: 814 us
  Pallas kernels  552 us (67%)
  waiting for transfers between devices  164 us (20%)
  matrix products  36.6 us (4%)
  local copies, waits for them, and re-layouts  27 us (3%)
  between operations  13.8 us (2%)
  starting transfers between devices  11.7 us (1%)
  other arithmetic  8.71 us (1%)
    pallas_call x1, Pallas kernels, local_layers(): pl.pallas_call(functools.partial(local_kernel, num_dev, num_layers), out_...  299 us
    all_gather x4, waiting for transfers between devices, per_device(): gathered.append(lax.all_gather(jnp.stack([k, v]), 'cp'))  146 us
    pallas_call x3, Pallas kernels, flat_heads(): pl.pallas_call(functools.partial(relayout_kernel, heads), grid=(layers, w...  136 us
    pallas_call x4, Pallas kernels, flash_head(): pl.pallas_call(functools.partial(flash_kernel, num_dev), out_shape=jax.Sh...  117 us
  transfers between devices with their start and end apart: 6, of which 6 were waited for; matrix products, arithmetic and copies ran while one was open for 5% of the time, Pallas kernels for 11%

profile of v1, /device:TPU:127, one launch (start us, length us, event | category | flops | bytes accessed | tf_op | source)
XLA Modules:
  0.0 813.6 jit_solution(2985613615453145721)
XLA Ops:
  6.6 38.3 %flat_heads.4.wk_hbm = bf16[6,2560,1024]{2,1,0:T(8,128)(2,1)} custom-call(bf16[256,256]{1,0:T(8,128)(2,1)} %constant.32.clone.perm, bf16[6,20480,128]{2,1,0:T(8,128)(2,1)} %bitcast.73), custom_call_target="tpu_custom_call" | custom-call | tf_op jit(solution)/shard_map/flat_heads/pallas_call | solution.py:54
  44.8 38.3 %flat_heads.5.wv_hbm = bf16[6,2560,1024]{2,1,0:T(8,128)(2,1)} custom-call(bf16[256,256]{1,0:T(8,128)(2,1)} %constant.32.clone.perm, bf16[6,20480,128]{2,1,0:T(8,128)(2,1)} %bitcast.74), custom_call_target="tpu_custom_call" | custom-call | tf_op jit(solution)/shard_map/flat_heads/pallas_call | solution.py:54
  83.2 5.3 slice_bitcast_fusion.3
  88.5 5.4 slice_bitcast_fusion.2
  93.9 59.0 %flat_heads.3.wq_hbm = bf16[6,2560,2048]{2,1,0:T(8,128)(2,1)} custom-call(bf16[256,256]{1,0:T(8,128)(2,1)} %constant.31.clone.perm, bf16[6,40960,128]{2,1,0:T(8,128)(2,1)} %bitcast.72), custom_call_target="tpu_custom_call" | custom-call | tf_op jit(solution)/shard_map/flat_heads/pallas_call | solution.py:54
  153.0 299.2 %local_layers.1 = bf16[512,2560]{1,0:T(8,128)(2,1)} custom-call(bf16[512,2560]{1,0:T(8,128)(2,1)} %x_in.1, bf16[6,2560,2048]{2,1,0:T(8,128)(2,1)} %flat_heads.3.wq_hbm, bf16[6,2560,1024]{2,1,0:T(8,128)(2,1)} %flat_heads.4.wk_hbm, bf16[6,2560,1024]{2,1,0:T(8,128)(2,1)} %flat_heads.5.wv_hbm, bf16[6,2048,2560]{2,1,0:T(8,128)(2,1)} %bitcast.71), custom_call_target="tpu_custom_call" | custom-call | tf_op jit(solution)/shard_map/local_layers/pallas_call | solution.py:270
  452.2 2.3 fusion.1
  454.5 3.1 fusion.78
  457.7 2.2 fusion.75
  461.0 2.2 fusion.72
  463.3 2.2 fusion.69
  466.4 2.2 fusion.66
  468.7 2.2 fusion.63
  471.9 2.2 fusion.60
  474.1 2.2 fusion.57
  478.9 7.0 collective-permute-start
  485.8 4.3 collective-permute-start.1
  490.2 8.6 %slice.78 = bf16[1,8,256,2560]{3,2,1,0:T(8,128)(2,1)} slice(bf16[6,8,256,2560]{3,2,1,0:T(8,128)(2,1)} %param.12), slice={[5:6], [0:8], [0:256], [0:2560]} | slice | bytes 20971520 | tf_op jit(solution)/shard_map/slice | solution.py:409
  498.8 3.9 collective-permute-done
  502.7 14.4 %collective-permute-done.1 = bf16[256,2560]{1,0:T(8,128)(2,1)S(1)} collective-permute-done((bf16[256,2560]{1,0:T(8,128)(2,1)}, bf16[256,2560]{1,0:T(8,128)(2,1)S(1)}, u32[]{:S(2)}, u32[]{:S(2)}) %collective-permute-start.1) | collective-permute-done | bytes 1310752 | tf_op jit(solution)/shard_map/ppermute | solution.py:370
  518.8 9.4 %fusion.6 = bf16[512,2048]{1,0:T(8,128)(2,1)} fusion(bf16[6,2560,2048]{2,1,0:T(8,128)(2,1)} %flat_heads.3.wq_hbm, f32[512]{0:T(512)S(1)} %add_rsqrt_fusion.2, bf16[256,2560]{1,0:T(8,128)(2,1)S(1)} %get-tuple-element.6, bf16[256,2560]{1,0:T(8,128)(2,1)S(1)} %get-tuple-element.5), kind=kOutput, calls=%fused_computation.15 | convolution fusion | flops 5377622016 | bytes 15206400 | tf_op jit(solution)/shard_map/dot_general | solution.py:402
  528.2 3.3 reshape.69
  533.3 27.0 %all-gather.9.cloned.1.call-done = bf16[64,512,256]{2,1,0:T(8,128)(2,1)} async-done(((bf16[2,512,256]{2,1,0:T(8,128)(2,1)}), bf16[64,512,256]{2,1,0:T(8,128)(2,1)}) %all-gather.9.cloned.1.call-update) | async-done | bytes 16777232 | tf_op jit(solution)/shard_map/all_gather | solution.py:399
  560.3 29.2 %flash_head.4 = bf16[512,512]{1,0:T(8,128)(2,1)S(1)} custom-call(bf16[2,512,256]{2,1,0:T(8,128)(2,1)S(1)} %bitcast.70, bf16[32,2,512,256]{3,2,1,0:T(8,128)(2,1)} %bitcast.76), custom_call_target="tpu_custom_call" | custom-call | flops 20000000000 | bytes 16000000 | tf_op jit(solution)/shard_map/flash_head/pallas_call | solution.py:350
  589.5 39.6 %all-gather.11.cloned.1.call-done = bf16[64,512,256]{2,1,0:T(8,128)(2,1)} async-done(((bf16[2,512,256]{2,1,0:T(8,128)(2,1)}), bf16[64,512,256]{2,1,0:T(8,128)(2,1)}) %all-gather.11.cloned.1.call-update) | async-done | bytes 16777232 | tf_op jit(solution)/shard_map/all_gather | solution.py:399
  629.1 29.2 %flash_head.5 = bf16[512,512]{1,0:T(8,128)(2,1)S(1)} custom-call(bf16[2,512,256]{2,1,0:T(8,128)(2,1)S(1)} %bitcast.69, bf16[32,2,512,256]{3,2,1,0:T(8,128)(2,1)} %bitcast.77), custom_call_target="tpu_custom_call" | custom-call | flops 20000000000 | bytes 16000000 | tf_op jit(solution)/shard_map/flash_head/pallas_call | solution.py:350
  658.3 39.6 %all-gather.13.cloned.1.call-done = bf16[64,512,256]{2,1,0:T(8,128)(2,1)} async-done(((bf16[2,512,256]{2,1,0:T(8,128)(2,1)}), bf16[64,512,256]{2,1,0:T(8,128)(2,1)}) %all-gather.13.cloned.1.call-update) | async-done | bytes 16777232 | tf_op jit(solution)/shard_map/all_gather | solution.py:399
  697.9 29.2 %flash_head.6 = bf16[512,512]{1,0:T(8,128)(2,1)S(1)} custom-call(bf16[2,512,256]{2,1,0:T(8,128)(2,1)S(1)} %bitcast.68, bf16[32,2,512,256]{3,2,1,0:T(8,128)(2,1)} %bitcast.78), custom_call_target="tpu_custom_call" | custom-call | flops 20000000000 | bytes 16000000 | tf_op jit(solution)/shard_map/flash_head/pallas_call | solution.py:350
  727.1 39.4 %all-gather.15.cloned.1.call-done = bf16[64,512,256]{2,1,0:T(8,128)(2,1)} async-done(((bf16[2,512,256]{2,1,0:T(8,128)(2,1)}), bf16[64,512,256]{2,1,0:T(8,128)(2,1)}) %all-gather.15.cloned.1.call-update) | async-done | bytes 16777232 | tf_op jit(solution)/shard_map/all_gather | solution.py:399
  766.6 29.2 %flash_head.7 = bf16[512,512]{1,0:T(8,128)(2,1)S(1)} custom-call(bf16[2,512,256]{2,1,0:T(8,128)(2,1)S(1)} %bitcast.67, bf16[32,2,512,256]{3,2,1,0:T(8,128)(2,1)} %bitcast.79), custom_call_target="tpu_custom_call" | custom-call | flops 20000000000 | bytes 16000000 | tf_op jit(solution)/shard_map/flash_head/pallas_call | solution.py:350
  795.8 8.7 %multiply_reduce_fusion = (f32[512]{0:T(512)S(1)}, f32[512,2560]{1,0:T(8,128)S(1)}) fusion(bf16[2048,2560]{1,0:T(8,128)(2,1)} %bitcast.75, bf16[512,512]{1,0:T(8,128)(2,1)S(1)} %flash_head.7, bf16[512,512]{1,0:T(8,128)(2,1)S(1)} %flash_head.6, bf16[512,512]{1,0:T(8,128)(2,1)S(1)} %flash_head.5, bf16[512,512]{1,0:T(8,128)(2,1)S(1)} %flash_head.4), kind=kOutput, calls=%fused_computation.14 | convolution fusion | flops 5379718656 | bytes 17827840 | tf_op jit(solution)/shard_map/dot_general | solution.py:409
  804.5 2.2 fusion.5
  (33 shorter events, 9.2 us)
Async XLA Ops:
  6.5 553.7 %all-gather.9.cloned.1.call-start = ((), (), s32[]{:S(2)}) async-start(), calls=%async_computation | async-start | bytes 17301504 | tf_op jit(solution)/shard_map/all_gather | solution.py:399
  454.5 3.2 copy-start
  460.8 168.3 %all-gather.11.cloned.1.call-start = ((), (), s32[]{:S(2)}) async-start(), calls=%async_computation.1 | async-start | bytes 17301504 | tf_op jit(solution)/shard_map/all_gather | solution.py:399
  466.4 231.5 %all-gather.13.cloned.1.call-start = ((), (), s32[]{:S(2)}) async-start(), calls=%async_computation.2 | async-start | bytes 17301504 | tf_op jit(solution)/shard_map/all_gather | solution.py:399
  471.8 294.8 %all-gather.15.cloned.1.call-start = ((), (), s32[]{:S(2)}) async-start(), calls=%async_computation.3 | async-start | bytes 17301504 | tf_op jit(solution)/shard_map/all_gather | solution.py:399
  478.9 23.8 %collective-permute-start = (bf16[256,2560]{1,0:T(8,128)(2,1)}, bf16[256,2560]{1,0:T(8,128)(2,1)S(1)}, u32[]{:S(2)}, u32[]{:S(2)}) collective-permute-start(bf16[256,2560]{1,0:T(8,128)(2,1)} %get-tuple-element.7), channel_id=1, source_target_pairs={{0,0},{1,2},{2,4},{3,6},{4,8},{5,10},{6,12},{7,14},{8,16},{9,18},{... | collective-permute-start | bytes 3932168 | tf_op jit(solution)/shard_map/ppermute | solution.py:369
  485.8 31.3 %collective-permute-start.1 = (bf16[256,2560]{1,0:T(8,128)(2,1)}, bf16[256,2560]{1,0:T(8,128)(2,1)S(1)}, u32[]{:S(2)}, u32[]{:S(2)}) collective-permute-start(bf16[256,2560]{1,0:T(8,128)(2,1)} %get-tuple-element.8), channel_id=1, source_target_pairs={{0,1},{1,3},{2,5},{3,7},{4,9},{5,11},{6,13},{7,15},{8,17},{9,19},{... | collective-permute-start | bytes 3932168 | tf_op jit(solution)/shard_map/ppermute | solution.py:370
  517.3 1.2 copy-start.1
  517.3 1.5 copy-start.3
  795.8 8.7 %copy-start.2 = (bf16[256,2560]{1,0:T(8,128)(2,1)S(1)}, bf16[256,2560]{1,0:T(8,128)(2,1)}, u32[]{:S(2)}) copy-start(bf16[256,2560]{1,0:T(8,128)(2,1)} %copy-done.1) | copy-start | bytes 3932164
  795.8 8.7 %copy-start.4 = (bf16[256,2560]{1,0:T(8,128)(2,1)S(1)}, bf16[256,2560]{1,0:T(8,128)(2,1)}, u32[]{:S(2)}) copy-start(bf16[256,2560]{1,0:T(8,128)(2,1)} %copy-done.3) | copy-start | bytes 3932164
Sparse Core Ops, SparseCore 0:
  460.9 99.3 all-gather.8
  562.4 66.6 all-gather.10
  631.2 66.6 all-gather.12
  699.8 66.6 all-gather.14

commit v2 on v1

v2 whole, which is shorter than its diff:
```python
import functools

import jax
import jax.numpy as jnp
import numpy as np
from jax import lax
from jax.experimental import pallas as pl
from jax.experimental.pallas import tpu as pltpu
from jax.sharding import PartitionSpec as P


EPS_NORM = 1e-6
NEG_BIG = -1e30
LOG2E = 1.4426950408889634
MESH = pl.DeviceIdType.MESH
NT = (((1,), (1,)), ((), ()))


def rms_normed(rows_in):
    widened = rows_in.astype(jnp.float32)
    return widened * lax.rsqrt(jnp.mean(widened * widened, axis=-1, keepdims=True) + EPS_NORM)


def iota2(shape, dim):
    return lax.broadcasted_iota(jnp.int32, shape, dim)


def perm_matrix(heads):
    dn = 128 // heads
    row = np.arange(256)
    h, ct, d = row // (2 * dn), (row // dn) % 2, row % dn
    out = np.zeros((256, 256), np.float32)
    out[row, d * 2 * heads + ct * heads + h] = 1
    return jnp.asarray(out, jnp.bfloat16)


def local_kernel(num_dev, num_layers, x_hbm, wq_hbm, wk_hbm, wv_hbm, wo_hbm, perm_q, perm_k, x_out, own_s,
                 n_s, q_s, halo_a, halo_b, o_s, acc, w_s, raw, wo_buf,
                 x_sem, raw_sem, o_sem, send_a, send_b, recv_a, recv_b, credit_a, credit_b):
    me = lax.axis_index("cp")
    odd = lax.rem(me, 2) == 1
    partner = jnp.where(odd, me - 1, me + 1)
    fwd = lax.rem(me + 2, num_dev)
    back = lax.rem(me + num_dev - 2, num_dev)
    rows, width = n_s.shape
    half = rows // 2
    kv_heads = own_s.shape[0]
    heads = 2 * kv_heads
    head = own_s.shape[-1]
    scale = head ** -0.5 * LOG2E
    slots, raw_rows, lanes = raw.shape
    dq, dk = raw_rows // (2 * heads), raw_rows // (2 * kv_heads)
    kv_chunks, q_chunks = 2 * width // dk, width // dq
    span = kv_chunks + q_chunks
    total_chunks = span * num_layers + kv_chunks

    barrier = pltpu.get_barrier_semaphore()
    for other in (fwd, back, partner):
        pl.semaphore_signal(barrier, inc=1, device_id={"cp": other}, device_id_type=MESH)
    pl.semaphore_wait(barrier, 3)

    def raw_copy(src, layer, i, g):
        slot = lax.rem(g, slots)
        part = pl.ds(pl.multiple_of(i * raw_rows, raw_rows), raw_rows)
        return pltpu.make_async_copy(src.at[layer, part], raw.at[slot], raw_sem.at[slot])

    def start_chunk(g):
        layer, i = g // span, lax.rem(g, span)

        @pl.when(jnp.logical_and(g < total_chunks, i < kv_chunks // 2))
        def _():
            raw_copy(wk_hbm, layer, i, g).start()

        @pl.when(jnp.logical_and(g < total_chunks, jnp.logical_and(i >= kv_chunks // 2, i < kv_chunks)))
        def _():
            raw_copy(wv_hbm, layer, i - kv_chunks // 2, g).start()

        @pl.when(jnp.logical_and(g < total_chunks, i >= kv_chunks))
        def _():
            raw_copy(wq_hbm, layer, i - kv_chunks, g).start()

    def flatten_chunk(layer, i, is_q):
        g = layer * span + i + (kv_chunks if is_q else 0)
        slot = lax.rem(g, slots)
        raw_copy(wk_hbm, 0, 0, g).wait()
        perm = perm_q if is_q else perm_k
        planes = heads if is_q else kv_heads
        dn = lanes // planes
        base = i * dq if is_q else lax.rem(i, kv_chunks // 2) * dk
        shift = 0 if is_q else pl.multiple_of(i // (kv_chunks // 2) * head, head)
        for b in range(raw_rows // 512):
            pair = jnp.concatenate([raw[slot, b * 512:b * 512 + 256, :], raw[slot, b * 512 + 256:b * 512 + 512, :]], axis=1)
            moved = jnp.dot(perm[...], pair, preferred_element_type=jnp.float32).astype(jnp.bfloat16)
            for h in range(planes):
                for ct in range(2):
                    row = (h * 2 + ct) * dn
                    for k in range(2):
                        part = pl.ds(pl.multiple_of(base + (2 * b + k) * dn, dn), dn)
                        piece = moved[row:row + dn, k * lanes:(k + 1) * lanes]
                        if is_q:
                            col = h % 2 * head + ct * lanes
                            w_s[h // 2, part, col:col + lanes] = piece
                        else:
                            w_s[h, part, pl.ds(pl.multiple_of(shift + ct * lanes, lanes), lanes)] = piece
        start_chunk(g + slots)

    def o_copy(layer, h):
        slot = lax.rem(h, 2)
        part = pl.ds(pl.multiple_of(h * 2 * head, 2 * head), 2 * head)
        return pltpu.make_async_copy(wo_hbm.at[layer, part], wo_buf.at[slot], o_sem.at[slot])

    x_copy = pltpu.make_async_copy(x_hbm, x_out, x_sem)
    x_copy.start()
    for g in range(slots):
        start_chunk(jnp.int32(g))
    for h in range(2):
        o_copy(0, h).start()

    def send_own(parity, h):
        return pltpu.make_async_remote_copy(
            src_ref=own_s.at[h], dst_ref=halo_a.at[parity, h], send_sem=send_a.at[h], recv_sem=recv_a.at[parity, h],
            device_id={"cp": fwd}, device_id_type=MESH)

    def send_partner(parity, h, src):
        return pltpu.make_async_remote_copy(
            src_ref=src, dst_ref=halo_b.at[parity, h], send_sem=send_b.at[h], recv_sem=recv_b.at[parity, h],
            device_id={"cp": partner}, device_id_type=MESH)

    def flatten_range(layer, lo, hi, is_q):
        def one(i, c):
            flatten_chunk(layer, i, is_q)
            return c

        lax.fori_loop(lo, hi, one, 0)

    x_copy.wait()

    def norm_rows(i, carry):
        part = pl.ds(pl.multiple_of(i * 32, 32), 32)
        n_s[part, :] = rms_normed(x_out[part, :]).astype(jnp.bfloat16)
        return carry

    lax.fori_loop(0, rows // 32, norm_rows, 0)
    flatten_range(0, 0, kv_chunks, False)

    bias_a = jnp.where(me < 2, NEG_BIG, 0.0)
    bias_b = jnp.where(me < 1, NEG_BIG, 0.0)

    def attend(parity, h, j):
        blocks = [(halo_a.at[parity, h], 0, bias_a), (halo_a.at[parity, h], 1, bias_a),
                  (halo_b.at[parity, h], 0, bias_b), (halo_b.at[parity, h], 1, bias_b),
                  (own_s.at[h], 0, None), (own_s.at[h], 1, None)][j:j + 5]
        q_tile = q_s[h, j]
        row = lax.rem(iota2((2 * half, half), 0), half)
        key = iota2((2 * half, half), 1)
        tiles = []
        for i, (ref, part, bias) in enumerate(blocks):
            keys = ref[0, part * half:(part + 1) * half, :]
            scores = lax.dot_general(q_tile, keys, NT, preferred_element_type=jnp.float32) * scale
            if bias is not None:
                scores = scores + bias
            if i == 0:
                scores = jnp.where(key > row, scores, NEG_BIG)
            if i == len(blocks) - 1:
                scores = jnp.where(key <= row, scores, NEG_BIG)
            tiles.append(scores)
        top = jnp.max(functools.reduce(jnp.maximum, tiles), axis=-1, keepdims=True)
        total, out = None, None
        for scores, (ref, part, _) in zip(tiles, blocks):
            e = jnp.exp2(scores - top)
            total = e if total is None else total + e
            term = jnp.dot(e.astype(jnp.bfloat16), ref[1, part * half:(part + 1) * half, :], preferred_element_type=jnp.float32)
            out = term if out is None else out + term
        out = (out / jnp.sum(total, axis=-1, keepdims=True)).astype(jnp.bfloat16)
        for g in range(2):
            o_s[j * half:(j + 1) * half, g * head:(g + 1) * head] = out[g * half:(g + 1) * half, :]

    def project_kv(h):
        kv = jnp.dot(n_s[...], w_s[h], preferred_element_type=jnp.float32).astype(jnp.bfloat16)
        own_s[h, 0] = kv[:, 0:head]
        own_s[h, 1] = kv[:, head:2 * head]

    def layer_step(layer, carry):
        parity = lax.rem(layer, 2)

        @pl.when(layer >= 2)
        def _():
            pl.semaphore_wait(credit_a, 1)
            pl.semaphore_wait(credit_b, 1)

        def kv_step(h, c):
            project_kv(h)
            send_own(parity, h).start()

            @pl.when(jnp.logical_not(odd))
            def _():
                send_partner(parity, h, own_s.at[h]).start()

            return c

        lax.fori_loop(0, kv_heads, kv_step, 0)
        flatten_range(layer, 0, q_chunks, True)

        def q_step(h, c):
            q = jnp.dot(n_s[...], w_s[h], preferred_element_type=jnp.float32).astype(jnp.bfloat16)
            for g in range(2):
                for j in range(2):
                    q_s[h, j, g * half:(g + 1) * half, :] = q[j * half:(j + 1) * half, g * head:(g + 1) * head]
            return c

        lax.fori_loop(0, kv_heads, q_step, 0)

        def attn_step(h, c):
            slot = lax.rem(h, 2)
            send_own(parity, h).wait_recv()

            @pl.when(odd)
            def _():
                send_partner(parity, h, halo_a.at[parity, h]).start()

            flatten_range(layer + 1, h * kv_chunks // kv_heads, (h + 1) * kv_chunks // kv_heads, False)
            send_partner(parity, h, own_s.at[h]).wait_recv()
            attend(parity, h, 0)
            attend(parity, h, 1)
            o_copy(layer, h).wait()

            def out_part(i, cc):
                cols = pl.ds(pl.multiple_of(i * 512, 512), 512)
                part = jnp.dot(o_s[...], wo_buf[slot, :, cols], preferred_element_type=jnp.float32)

                @pl.when(h == 0)
                def _():
                    acc[:, cols] = part

                @pl.when(h > 0)
                def _():
                    acc[:, cols] = acc[:, cols] + part

                return cc

            lax.fori_loop(0, width // 512, out_part, 0)

            @pl.when(h < kv_heads - 2)
            def _():
                o_copy(layer, h + 2).start()

            @pl.when(jnp.logical_and(h >= kv_heads - 2, layer < num_layers - 1))
            def _():
                o_copy(layer + 1, h + 2 - kv_heads).start()

            return c

        lax.fori_loop(0, kv_heads, attn_step, 0)

        def drain(h, c):
            send_own(parity, h).wait_send()
            send_partner(parity, h, own_s.at[h]).wait_send()
            return c

        lax.fori_loop(0, kv_heads, drain, 0)

        @pl.when(layer < num_layers - 2)
        def _():
            pl.semaphore_signal(credit_a, inc=1, device_id={"cp": back}, device_id_type=MESH)
            pl.semaphore_signal(credit_b, inc=1, device_id={"cp": partner}, device_id_type=MESH)

        def update_rows(i, c):
            part = pl.ds(pl.multiple_of(i * 32, 32), 32)
            fresh = (x_out[part, :].astype(jnp.float32) + rms_normed(acc[part, :])).astype(jnp.bfloat16)
            x_out[part, :] = fresh
            n_s[part, :] = rms_normed(fresh).astype(jnp.bfloat16)
            return c

        lax.fori_loop(0, rows // 32, update_rows, 0)
        return carry

    lax.fori_loop(0, num_layers, layer_step, 0)

    def last_kv(h, c):
        project_kv(h)
        return c

    lax.fori_loop(0, kv_heads, last_kv, 0)


def tile_rows(w):
    layers, width, heads, _ = w.shape
    return w.reshape(layers, width, heads, 2, 128).transpose(0, 1, 3, 2, 4).reshape(layers, width * 2 * heads, 128)


def local_layers(hidden, w_query, w_key, w_value, w_out, num_dev, num_layers):
    rows, width = hidden.shape
    heads, head = w_query.shape[2:]
    kv_heads = w_key.shape[2]
    half = rows // 2
    bf16, f32 = jnp.bfloat16, jnp.float32
    hbm = pl.BlockSpec(memory_space=pltpu.HBM)
    vmem = pl.BlockSpec(memory_space=pltpu.VMEM)
    dma = pltpu.SemaphoreType.DMA
    return pl.pallas_call(
        functools.partial(local_kernel, num_dev, num_layers),
        out_shape=(jax.ShapeDtypeStruct((rows, width), bf16), jax.ShapeDtypeStruct((kv_heads, 2, rows, head), bf16)),
        in_specs=[hbm, hbm, hbm, hbm, hbm, vmem, vmem],
        out_specs=(vmem, vmem),
        scratch_shapes=[
            pltpu.VMEM((rows, width), bf16),
            pltpu.VMEM((kv_heads, 2, 2 * half, head), bf16),
            pltpu.VMEM((2, kv_heads, 2, rows, head), bf16),
            pltpu.VMEM((2, kv_heads, 2, rows, head), bf16),
            pltpu.VMEM((rows, 2 * head), bf16),
            pltpu.VMEM((rows, width), f32),
            pltpu.VMEM((kv_heads, width, 2 * head), bf16),
            pltpu.VMEM((4, 4096, 128), bf16),
            pltpu.VMEM((2, 2 * head, width), bf16),
            dma, dma((4,)), dma((2,)),
            dma((kv_heads,)), dma((kv_heads,)), dma((2, kv_heads)), dma((2, kv_heads)),
            pltpu.SemaphoreType.REGULAR, pltpu.SemaphoreType.REGULAR,
        ],
        compiler_params=pltpu.CompilerParams(collective_id=0, has_side_effects=True, vmem_limit_bytes=62 * 1024 * 1024),
        name="local_layers",
    )(hidden, tile_rows(w_query), tile_rows(w_key), tile_rows(w_value), w_out, perm_matrix(heads), perm_matrix(kv_heads))


def output_kernel(attn, w, x, out, acc):
    i = pl.program_id(0)
    part = jnp.dot(attn[...], w[0], preferred_element_type=jnp.float32)

    @pl.when(i == 0)
    def _():
        acc[...] = part

    @pl.when(i > 0)
    def _():
        acc[...] = acc[...] + part

    @pl.when(i == pl.num_programs(0) - 1)
    def _():
        out[...] = (x[...].astype(jnp.float32) + rms_normed(acc[...])).astype(jnp.bfloat16)


def output_update(hidden, outs, w_out, layer):
    rows, width = hidden.shape
    attn = jnp.concatenate(outs, axis=1)
    depth = attn.shape[1] // 4
    return pl.pallas_call(
        output_kernel,
        grid=(4,),
        in_specs=[pl.BlockSpec((rows, depth), lambda i: (0, i)), pl.BlockSpec((1, depth, width), lambda i: (layer, i, 0)),
                  pl.BlockSpec((rows, width), lambda i: (0, 0))],
        out_specs=pl.BlockSpec((rows, width), lambda i: (0, 0)),
        out_shape=jax.ShapeDtypeStruct((rows, width), jnp.bfloat16),
        scratch_shapes=[pltpu.VMEM((rows, width), jnp.float32)],
        name="output_update",
    )(attn, w_out, hidden)


def flash_kernel(num_dev, which, q_ref, kv_hbm, out_ref, kv_buf, acc, m_s, l_s, s_a, s_b, sems):
    nch = kv_buf.shape[0]
    me = lax.axis_index("cp")
    half = q_ref.shape[1] // 2
    head = q_ref.shape[2]
    scale = head ** -0.5 * LOG2E
    num_rows = q_ref.shape[1]
    step_keys = kv_buf.shape[2]
    blocks = (me, 2 * num_dev - 1 - me)
    need = [(b * half + half + step_keys - 1) // step_keys for b in blocks]
    copies=lambda c: pltpu.make_async_copy(kv_hbm.at[c, which], kv_buf.at[c], sems.at[c])

    def start(c, carry):
        copies(c).start(); return carry

    lax.fori_loop(0, need[1], start, 0)
    m_s[...] = jnp.full(m_s.shape, NEG_BIG, jnp.float32)
    l_s[...] = jnp.zeros(l_s.shape, jnp.float32)
    acc[...] = jnp.zeros(acc.shape, jnp.float32)
    total = num_dev + 1

    def where(t):
        trail = t < need[1]
        b = jnp.where(trail, 1, 0)
        c = jnp.where(trail, t, t - need[1])
        return b, jnp.minimum(c, nch - 1)

    def qk(t, dst):
        b, c = where(t)
        dst[...] = lax.dot_general(q_ref[b], kv_buf[c, 0], NT, preferred_element_type=jnp.float32) * scale

    def soft(t, src, nxt, dst, masked):
        if dst is not None:
            qk(nxt, dst)
        b, c = where(t)
        s = src[...]
        if masked:
            row = jnp.where(b == 1, blocks[1], blocks[0]) * half + lax.rem(iota2((num_rows, step_keys), 0), half)
            key = c * step_keys + iota2((num_rows, step_keys), 1)
            s = jnp.where(key <= row, s, NEG_BIG)
        old = m_s[b]
        top = jnp.maximum(old, jnp.max(s, axis=-1, keepdims=True))
        e = jnp.exp2(s - jnp.concatenate([top] * (step_keys // 128), axis=1))
        fix = jnp.exp2(old - top)
        m_s[b] = top
        part = e[:, 0:128]
        for i in range(1, step_keys // 128):
            part = part + e[:, i * 128:(i + 1) * 128]
        l_s[b] = l_s[b] * fix + part
        acc[b] = acc[b] * jnp.concatenate([fix] * (head // 128), axis=1) + jnp.dot(e.astype(jnp.bfloat16), kv_buf[c, 1], preferred_element_type=jnp.float32)

    def tile(t, src, dst):
        nxt = t + 1

        @pl.when(nxt < need[1])
        def _():
            copies(nxt).wait()

        edge = jnp.logical_or(t == need[1] - 1, t == total - 1)

        @pl.when(edge)
        def _():
            soft(t, src, nxt, dst, True)

        @pl.when(jnp.logical_not(edge))
        def _():
            soft(t, src, nxt, dst, False)

    copies(0).wait()
    qk(0, s_a)

    def pair(u, carry):
        tile(2 * u, s_a, s_b)
        tile(2 * u + 1, s_b, s_a)
        return carry

    lax.fori_loop(0, (total - 1) // 2, pair, 0)
    soft(total - 1, s_a, None, None, True)
    for b in range(2):
        inv = 1.0 / jnp.sum(l_s[b],axis=-1,keepdims=True)
        out = (acc[b] * inv).astype(jnp.bfloat16)
        for g in range(2):
            out_ref[b * half:(b + 1) * half, g * head:(g + 1) * head] = out[g * half:(g + 1) * half]


def flash_head(queries, kv_all, which, num_dev):
    _, num_rows, head = queries.shape
    half = num_rows // 2
    f32 = jnp.float32
    nch, tok = kv_all.shape[0], kv_all.shape[3]
    return pl.pallas_call(
        functools.partial(flash_kernel, num_dev, which),
        out_shape=jax.ShapeDtypeStruct((2 * half, 2 * head), jnp.bfloat16),
        in_specs=[pl.BlockSpec(memory_space=pltpu.VMEM), pl.BlockSpec(memory_space=pltpu.HBM)],
        out_specs=pl.BlockSpec(memory_space=pltpu.VMEM),
        scratch_shapes=[pltpu.VMEM((nch, 2, tok, head), jnp.bfloat16), pltpu.VMEM((2, num_rows, head), f32),
            pltpu.VMEM((2, num_rows, 128), f32), pltpu.VMEM((2, num_rows, 128), f32), pltpu.VMEM((num_rows, tok), f32), pltpu.VMEM((num_rows, tok), f32), pltpu.SemaphoreType.DMA((nch,))],
        compiler_params=pltpu.CompilerParams(vmem_limit_bytes=48 * 1024 * 1024),
        cost_estimate=pl.CostEstimate(flops=20_000_000_000, bytes_accessed=16_000_000, transcendentals=0), name="flash_head")(queries, kv_all)


def output_owner(block_idx, num_dev):
    return block_idx if block_idx < num_dev else 2 * num_dev - 1 - block_idx


def to_output_layout(hidden, dev_rank, num_dev):
    block_len = hidden.shape[0] // 2
    even_pairs = [(source, output_owner(2 * source, num_dev)) for source in range(num_dev)]
    odd_pairs = [(source, output_owner(2 * source + 1, num_dev)) for source in range(num_dev)]
    from_even = lax.ppermute(hidden[:block_len], "cp", even_pairs)
    from_odd = lax.ppermute(hidden[block_len:], "cp", odd_pairs)
    is_even = dev_rank % 2 == 0
    lead_rows = jnp.where(is_even, from_even, from_odd)
    trail_rows = jnp.where(is_even, from_odd, from_even)
    return jnp.concatenate([lead_rows, trail_rows], axis=0)


def solution(mesh):
    num_dev = mesh.shape["cp"]

    def per_device(hidden, w_query, w_key, w_value, w_out):
        dev_rank = lax.axis_index("cp")
        layers, width, heads, head = w_query.shape
        kv_heads = w_key.shape[2]
        group = heads // kv_heads
        wo = w_out.reshape(layers, heads * head, width)
        last = layers - 1
        hidden, kv = local_layers(hidden, w_query, w_key, w_value, wo, num_dev, last)
        half = hidden.shape[0] // 2
        cuts = [0, kv_heads - 1, kv_heads]
        most = lax.all_gather(kv[:cuts[1]], "cp")
        rest = lax.all_gather(kv[cuts[1]:], "cp")
        hidden = to_output_layout(hidden, dev_rank, num_dev)
        gathered = [most, rest]
        normed = rms_normed(hidden).astype(jnp.bfloat16)
        queries = jnp.einsum("td,dhe->the", normed, w_query[last], preferred_element_type=jnp.float32).astype(jnp.bfloat16)
        queries = queries.reshape(2, half, kv_heads, group, head)
        outs = []
        for lo, hi, kv_all in zip(cuts, cuts[1:], gathered):
            for h in range(lo, hi):
                q = jnp.transpose(queries[:, :, h], (0, 2, 1, 3)).reshape(2, group * half, head)
                outs.append(flash_head(q, kv_all, h - lo, num_dev))
        return output_update(hidden, outs, wo, last)

    row_spec = P(("dp", "cp"), None)
    return jax.shard_map(per_device, mesh=mesh, in_specs=(row_spec, P(), P(), P(), P()), out_specs=row_spec, check_vma=False)
```

time: 829 us -> 651 us (0.79); the launches traced: 814 us -> 646 us
  Pallas kernels: 552 us -> 398 us
  waiting for transfers between devices: 164 us -> 195 us
  matrix products: 36.6 us -> 8.41 us
  local copies, waits for them, and re-layouts: 27 us -> 16.6 us
    pallas_call x7 -> x5, Pallas kernels: 253 us -> 91 us  [the longest x4 77.3 us: flash_head(): pl.pallas_call(functools.partial(flash_kernel, num_dev, which), out_shape...]
    dot_general x10 -> x1, matrix products: 36.6 us -> 8.41 us  [per_device(): jnp.einsum('td,dhe->the', normed, w_query[last], preferred_element_type=j...]
    all_gather x4 -> x2, waiting for transfers between devices: 146 us -> 169 us  [the longest x1 134 us: per_device(): most = lax.all_gather(kv[:cuts[1]], 'cp')]
    squeeze x2 -> x0, local copies, waits for them, and re-layouts: 10.8 us -> none  [the longest x1 5.41 us: per_device(): wv[last][:, cols]]
  transfers between devices with their start and end apart: 6 -> 4, of which waited for: 6 -> 4; matrix products, arithmetic and copies ran while one was open for 5% -> 4% of each run, Pallas kernels for 11% -> 3%
where the time goes in v2:
time: 651 us; the launch traced here: 646 us
  Pallas kernels  398 us (61%)
  waiting for transfers between devices  195 us (30%)
  local copies, waits for them, and re-layouts  16.6 us (3%)
  between operations  13.5 us (2%)
  starting transfers between devices  9.77 us (2%)
  matrix products  8.41 us (1%)
    pallas_call x1, Pallas kernels, local_layers(): pl.pallas_call(functools.partial(local_kernel, num_dev, num_layers), out_...  307 us
    all_gather x1, waiting for transfers between devices, per_device(): most = lax.all_gather(kv[:cuts[1]], 'cp')  134 us
    pallas_call x4, Pallas kernels, flash_head(): pl.pallas_call(functools.partial(flash_kernel, num_dev, which), out_shape...  77.3 us
    all_gather x1, waiting for transfers between devices, per_device(): rest = lax.all_gather(kv[cuts[1]:], 'cp')  34.3 us
    ppermute x1, waiting for transfers between devices, to_output_layout(): from_odd = lax.ppermute(hidden[block_len:], 'cp', odd_pairs)  15.6 us
    pallas_call x1, Pallas kernels, output_update(): pl.pallas_call(output_kernel, grid=(4,), in_specs=[pl.BlockSpec((rows, de...  13.7 us
  transfers between devices with their start and end apart: 4, of which 4 were waited for; matrix products, arithmetic and copies ran while one was open for 4% of the time, Pallas kernels for 3%

profile of v2, /device:TPU:127, one launch (start us, length us, event | category | flops | bytes accessed | tf_op | source)
XLA Modules:
  0.0 646.0 jit_solution(11174708629919292478)
XLA Ops:
  6.5 0.0 all-gather.7.cloned.1.call-start
  6.6 307.1 %local_layers.1 = (bf16[512,2560]{1,0:T(8,128)(2,1)}, bf16[4,2,512,256]{3,2,1,0:T(8,128)(2,1)}) custom-call(bf16[512,2560]{1,0:T(8,128)(2,1)} %x_hbm.1, bf16[6,40960,128]{2,1,0:T(8,128)(2,1)} %bitcast.55, bf16[6,20480,128]{2,1,0:T(8,128)(2,1)} %bitcast.56, bf16[6,20480,128]{2,1,0:T(8,128)(2,1)} %bitcast.57, bf16[6,2048,2560]{2,1,0:T(8,128)(2,1)} %bitcast.53, ...), custom_call_target="tpu_custom_call" | custom-call | tf_op jit(solution)/shard_map/local_layers/pallas_call | solution.py:300
  313.6 1.9 slice.35
  315.5 0.0 copy-start
  315.5 0.1 all-gather.7.cloned.1.call-update
  315.6 0.1 all-gather.5.cloned.1.call-start
  315.7 2.8 slice.31
  318.5 0.1 all-gather.5.cloned.1.call-update
  318.5 0.0 copy-done
  318.5 1.7 fusion.9
  320.3 5.9 collective-permute-start
  326.2 3.8 collective-permute-start.1
  330.0 9.8 %slice.29 = bf16[1,2560,8,256]{3,2,1,0:T(8,128)(2,1)} slice(bf16[6,2560,8,256]{3,2,1,0:T(8,128)(2,1)} %param.8), slice={[5:6], [0:2560], [0:8], [0:256]} | slice | bytes 20971520 | tf_op jit(solution)/shard_map/slice | solution.py:492
  339.8 11.1 %collective-permute-done = bf16[256,2560]{1,0:T(8,128)(2,1)S(1)} collective-permute-done((bf16[256,2560]{1,0:T(8,128)(2,1)}, bf16[256,2560]{1,0:T(8,128)(2,1)S(1)}, u32[]{:S(2)}, u32[]{:S(2)}) %collective-permute-start) | collective-permute-done | bytes 1310752 | tf_op jit(solution)/shard_map/ppermute | solution.py:466
  350.9 15.6 %collective-permute-done.1 = bf16[256,2560]{1,0:T(8,128)(2,1)S(1)} collective-permute-done((bf16[256,2560]{1,0:T(8,128)(2,1)}, bf16[256,2560]{1,0:T(8,128)(2,1)S(1)}, u32[]{:S(2)}, u32[]{:S(2)}) %collective-permute-start.1) | collective-permute-done | bytes 1310752 | tf_op jit(solution)/shard_map/ppermute | solution.py:467
  366.4 0.2 broadcast_select_fusion.1
  366.6 0.6 fusion.1
  367.2 8.4 %fusion.6 = bf16[512,8,256]{2,0,1:T(8,128)(2,1)S(1)} fusion(bf16[1,2560,8,256]{3,2,1,0:T(8,128)(2,1)} %slice.29, f32[512]{0:T(512)S(1)} %add_rsqrt_fusion, bf16[256,2560]{1,0:T(8,128)(2,1)S(1)} %get-tuple-element.10, bf16[256,2560]{1,0:T(8,128)(2,1)S(1)} %get-tuple-element.9), kind=kOutput, calls=%fused_computation.10 | convolution fusion | flops 5377622016 | bytes 15206400 | tf_op jit(solution)/shard_map/td,dhe->the/dot_general | solution.py:492
  375.6 0.1 fusion.10
  376.0 1.7 pad_maximum_fusion.x
  377.7 34.3 %all-gather.7.cloned.1.call-done = bf16[32,2,512,256]{3,2,1,0:T(8,128)(2,1)} async-done(((bf16[1,2,512,256]{3,2,1,0:T(8,128)(2,1)}), bf16[32,2,512,256]{3,2,1,0:T(8,128)(2,1)}) %all-gather.7.cloned.1.call-update) | async-done | bytes 16777232 | tf_op jit(solution)/shard_map/all_gather | solution.py:488
  412.0 19.3 %flash_head.7 = bf16[512,512]{1,0:T(8,128)(2,1)S(1)} custom-call(bf16[2,512,256]{2,1,0:T(8,128)(2,1)S(1)} %bitcast.52, bf16[32,1,2,512,256]{4,3,2,1,0:T(8,128)(2,1)} %bitcast.62), custom_call_target="tpu_custom_call" | custom-call | flops 20000000000 | bytes 16000000 | tf_op jit(solution)/shard_map/flash_head/pallas_call | solution.py:447
  431.3 134.4 %all-gather.5.cloned.1.call-done = bf16[96,2,512,256]{3,2,1,0:T(8,128)(2,1)} async-done(((bf16[3,2,512,256]{3,2,1,0:T(8,128)(2,1)}), bf16[96,2,512,256]{3,2,1,0:T(8,128)(2,1)}) %all-gather.5.cloned.1.call-update) | async-done | bytes 50331664 | tf_op jit(solution)/shard_map/all_gather | solution.py:487
  565.7 19.3 %flash_head.6 = bf16[512,512]{1,0:T(8,128)(2,1)S(1)} custom-call(bf16[2,512,256]{2,1,0:T(8,128)(2,1)S(1)} %bitcast.49, bf16[32,3,2,512,256]{4,3,2,1,0:T(8,128)(2,1)} %bitcast.59), custom_call_target="tpu_custom_call" | custom-call | flops 20000000000 | bytes 16000000 | tf_op jit(solution)/shard_map/flash_head/pallas_call | solution.py:447
  585.0 19.3 %flash_head.5 = bf16[512,512]{1,0:T(8,128)(2,1)S(1)} custom-call(bf16[2,512,256]{2,1,0:T(8,128)(2,1)S(1)} %bitcast.50, bf16[32,3,2,512,256]{4,3,2,1,0:T(8,128)(2,1)} %bitcast.60), custom_call_target="tpu_custom_call" | custom-call | flops 20000000000 | bytes 16000000 | tf_op jit(solution)/shard_map/flash_head/pallas_call | solution.py:447
  604.4 19.3 %flash_head.4 = bf16[512,512]{1,0:T(8,128)(2,1)S(1)} custom-call(bf16[2,512,256]{2,1,0:T(8,128)(2,1)S(1)} %bitcast.51, bf16[32,3,2,512,256]{4,3,2,1,0:T(8,128)(2,1)} %bitcast.61), custom_call_target="tpu_custom_call" | custom-call | flops 20000000000 | bytes 16000000 | tf_op jit(solution)/shard_map/flash_head/pallas_call | solution.py:447
  623.7 1.6 pad_maximum_fusion.1.attn
  625.4 13.7 %output_update.1 = bf16[512,2560]{1,0:T(8,128)(2,1)} custom-call(bf16[512,2048]{1,0:T(8,128)(2,1)} %pad_maximum_fusion.1.attn, bf16[6,2048,2560]{2,1,0:T(8,128)(2,1)} %bitcast.54, bf16[512,2560]{1,0:T(8,128)(2,1)} %pad_maximum_fusion.x), custom_call_target="tpu_custom_call" | custom-call | tf_op jit(solution)/shard_map/output_update/pallas_call | solution.py:345
  (5 shorter events, 0.2 us)
Async XLA Ops:
  6.5 405.4 %all-gather.7.cloned.1.call-start = ((), (), s32[]{:S(2)}) async-start(), calls=%async_computation.1 | async-start | bytes 17301504 | tf_op jit(solution)/shard_map/all_gather | solution.py:488
  315.5 3.0 copy-start
  315.6 250.1 %all-gather.5.cloned.1.call-start = ((), (), s32[]{:S(2)}) async-start(), calls=%async_computation | async-start | bytes 51904512 | tf_op jit(solution)/shard_map/all_gather | solution.py:487
  320.3 30.6 %collective-permute-start = (bf16[256,2560]{1,0:T(8,128)(2,1)}, bf16[256,2560]{1,0:T(8,128)(2,1)S(1)}, u32[]{:S(2)}, u32[]{:S(2)}) collective-permute-start(bf16[256,2560]{1,0:T(8,128)(2,1)} %get-tuple-element.11), channel_id=1, source_target_pairs={{0,0},{1,2},{2,4},{3,6},{4,8},{5,10},{6,12},{7,14},{8,16},{9,18},{... | collective-permute-start | bytes 3932168 | tf_op jit(solution)/shard_map/ppermute | solution.py:466
  326.2 40.2 %collective-permute-start.1 = (bf16[256,2560]{1,0:T(8,128)(2,1)}, bf16[256,2560]{1,0:T(8,128)(2,1)S(1)}, u32[]{:S(2)}, u32[]{:S(2)}) collective-permute-start(bf16[256,2560]{1,0:T(8,128)(2,1)} %get-tuple-element.12), channel_id=1, source_target_pairs={{0,1},{1,3},{2,5},{3,7},{4,9},{5,11},{6,13},{7,15},{8,17},{9,19},{... | collective-permute-start | bytes 3932168 | tf_op jit(solution)/shard_map/ppermute | solution.py:467
Sparse Core Ops, SparseCore 0:
  315.7 96.1 all-gather.6
  414.0 151.6 all-gather.4

commit v3 on v2

--- a/solution.py
+++ b/solution.py
@@ -1,4 +1,5 @@
 import functools
+import math
 
 import jax
 import jax.numpy as jnp
@@ -35,16 +36,28 @@
 
 
 def local_kernel(num_dev, num_layers, x_hbm, wq_hbm, wk_hbm, wv_hbm, wo_hbm, perm_q, perm_k, x_out, own_s,
-                 n_s, q_s, halo_a, halo_b, o_s, acc, w_s, raw, wo_buf,
-                 x_sem, raw_sem, o_sem, send_a, send_b, recv_a, recv_b, credit_a, credit_b):
+                 n_s, q_s, halo_a, halo_b, o_s, acc, w_s, raw, wo_buf, relay_1, relay_2, s_a, s_b,
+                 x_sem, raw_sem, o_sem, send_a, send_b, recv_a, recv_b, send_r, recv_r, credit_a, credit_b, credit_r, credit_t):
     me = lax.axis_index("cp")
     odd = lax.rem(me, 2) == 1
     partner = jnp.where(odd, me - 1, me + 1)
     fwd = lax.rem(me + 2, num_dev)
     back = lax.rem(me + num_dev - 2, num_dev)
+    ring = math.isqrt(num_dev // 2)
+    chips = num_dev // 2
+    chip, core = me // 2, lax.rem(me, 2)
+
+    def ring_dev(c, shift):
+        base = c // ring * ring
+        return 2 * (base + lax.rem(c - base + ring + shift, ring)) + core
+
+    left, right = ring_dev(chip, -1), ring_dev(chip, 1)
+    target = 2 * lax.rem(ring_dev(chip, 2) // 2 + 1, chips) + core
+    writer = ring_dev(lax.rem(chip + chips - 1, chips), -2)
     rows, width = n_s.shape
     half = rows // 2
     kv_heads = own_s.shape[0]
+    relayed = kv_heads - 1
     heads = 2 * kv_heads
     head = own_s.shape[-1]
     scale = head ** -0.5 * LOG2E
@@ -55,9 +68,9 @@
     total_chunks = span * num_layers + kv_chunks
 
     barrier = pltpu.get_barrier_semaphore()
-    for other in (fwd, back, partner):
+    for other in (fwd, back, partner, left, right, target, writer):
         pl.semaphore_signal(barrier, inc=1, device_id={"cp": other}, device_id_type=MESH)
-    pl.semaphore_wait(barrier, 3)
+    pl.semaphore_wait(barrier, 7)
 
     def raw_copy(src, layer, i, g):
         slot = lax.rem(g, slots)
@@ -104,17 +117,20 @@
                             w_s[h, part, pl.ds(pl.multiple_of(shift + ct * lanes, lanes), lanes)] = piece
         start_chunk(g + slots)
 
-    def o_copy(layer, h):
-        slot = lax.rem(h, 2)
-        part = pl.ds(pl.multiple_of(h * 2 * head, 2 * head), 2 * head)
+    def head_at(i):
+        return jnp.where(i < kv_heads - 2, i, 2 * kv_heads - 3 - i)
+
+    def o_copy(layer, i):
+        slot = lax.rem(i, 2)
+        part = pl.ds(pl.multiple_of(head_at(i) * 2 * head, 2 * head), 2 * head)
         return pltpu.make_async_copy(wo_hbm.at[layer, part], wo_buf.at[slot], o_sem.at[slot])
 
     x_copy = pltpu.make_async_copy(x_hbm, x_out, x_sem)
     x_copy.start()
     for g in range(slots):
         start_chunk(jnp.int32(g))
-    for h in range(2):
-        o_copy(0, h).start()
+    for i in range(2):
+        o_copy(0, jnp.int32(i)).start()
 
     def send_own(parity, h):
         return pltpu.make_async_remote_copy(
@@ -126,6 +142,17 @@
             src_ref=src, dst_ref=halo_b.at[parity, h], send_sem=send_b.at[h], recv_sem=recv_b.at[parity, h],
             device_id={"cp": partner}, device_id_type=MESH)
 
+    def hop(parity, leg, kv):
+        src = (own_s.at[relayed, kv], relay_1.at[parity, kv], relay_2.at[parity, kv])[leg]
+        dst = (relay_1.at[parity, kv], relay_2.at[parity, kv], halo_a.at[parity, relayed, kv])[leg]
+        return pltpu.make_async_remote_copy(
+            src_ref=src, dst_ref=dst, send_sem=send_r.at[leg, kv], recv_sem=recv_r.at[parity, leg, kv],
+            device_id={"cp": (left, left, target)[leg]}, device_id_type=MESH)
+
+    def pass_on(parity, leg, kv):
+        hop(parity, leg, kv).wait_recv()
+        hop(parity, leg + 1, kv).start()
+
     def flatten_range(layer, lo, hi, is_q):
         def one(i, c):
             flatten_chunk(layer, i, is_q)
@@ -146,34 +173,42 @@
     bias_a = jnp.where(me < 2, NEG_BIG, 0.0)
     bias_b = jnp.where(me < 1, NEG_BIG, 0.0)
 
-    def attend(parity, h, j):
-        blocks = [(halo_a.at[parity, h], 0, bias_a), (halo_a.at[parity, h], 1, bias_a),
-                  (halo_b.at[parity, h], 0, bias_b), (halo_b.at[parity, h], 1, bias_b),
-                  (own_s.at[h], 0, None), (own_s.at[h], 1, None)][j:j + 5]
-        q_tile = q_s[h, j]
-        row = lax.rem(iota2((2 * half, half), 0), half)
-        key = iota2((2 * half, half), 1)
-        tiles = []
-        for i, (ref, part, bias) in enumerate(blocks):
-            keys = ref[0, part * half:(part + 1) * half, :]
-            scores = lax.dot_general(q_tile, keys, NT, preferred_element_type=jnp.float32) * scale
-            if bias is not None:
-                scores = scores + bias
-            if i == 0:
-                scores = jnp.where(key > row, scores, NEG_BIG)
-            if i == len(blocks) - 1:
-                scores = jnp.where(key <= row, scores, NEG_BIG)
-            tiles.append(scores)
-        top = jnp.max(functools.reduce(jnp.maximum, tiles), axis=-1, keepdims=True)
-        total, out = None, None
-        for scores, (ref, part, _) in zip(tiles, blocks):
-            e = jnp.exp2(scores - top)
-            total = e if total is None else total + e
-            term = jnp.dot(e.astype(jnp.bfloat16), ref[1, part * half:(part + 1) * half, :], preferred_element_type=jnp.float32)
-            out = term if out is None else out + term
-        out = (out / jnp.sum(total, axis=-1, keepdims=True)).astype(jnp.bfloat16)
-        for g in range(2):
-            o_s[j * half:(j + 1) * half, g * head:(g + 1) * head] = out[g * half:(g + 1) * half, :]
+    def attend(parity, h):
+        row, key = iota2((half, half), 0), iota2((half, half), 1)
+        units = [(j, g, (s_a, s_b)[j].at[g * half:(g + 1) * half]) for j in range(2) for g in range(2)]
+
+        def blocks_of(j):
+            return [(halo_a.at[parity, h], 0, bias_a), (halo_a.at[parity, h], 1, bias_a),
+                    (halo_b.at[parity, h], 0, bias_b), (halo_b.at[parity, h], 1, bias_b),
+                    (own_s.at[h], 0, None), (own_s.at[h], 1, None)][j:j + 5]
+
+        def score(j, g, buf):
+            q_tile = q_s[h, j, g * half:(g + 1) * half, :]
+            for i, (ref, part, bias) in enumerate(blocks_of(j)):
+                keys = ref[0, part * half:(part + 1) * half, :]
+                scores = lax.dot_general(q_tile, keys, NT, preferred_element_type=jnp.float32) * scale
+                if bias is not None:
+                    scores = scores + bias
+                if i == 0:
+                    scores = jnp.where(key > row, scores, NEG_BIG)
+                if i == 4:
+                    scores = jnp.where(key <= row, scores, NEG_BIG)
+                buf[:, i * half:(i + 1) * half] = scores
+
+        score(*units[0])
+        for u, (j, g, buf) in enumerate(units):
+            if u + 1 < len(units):
+                score(*units[u + 1])
+            tiles = [buf[:, i * half:(i + 1) * half] for i in range(5)]
+            top = jnp.max(functools.reduce(jnp.maximum, tiles), axis=-1, keepdims=True)
+            total, out = None, None
+            for scores, (ref, part, _) in zip(tiles, blocks_of(j)):
+                e = jnp.exp2(scores - top)
+                total = e if total is None else total + e
+                term = jnp.dot(e.astype(jnp.bfloat16), ref[1, part * half:(part + 1) * half, :], preferred_element_type=jnp.float32)
+                out = term if out is None else out + term
+            out = (out / jnp.sum(total, axis=-1, keepdims=True)).astype(jnp.bfloat16)
+            o_s[j * half:(j + 1) * half, g * head:(g + 1) * head] = out
 
     def project_kv(h):
         kv = jnp.dot(n_s[...], w_s[h], preferred_element_type=jnp.float32).astype(jnp.bfloat16)
@@ -187,10 +222,21 @@
         def _():
             pl.semaphore_wait(credit_a, 1)
             pl.semaphore_wait(credit_b, 1)
-
-        def kv_step(h, c):
+            pl.semaphore_wait(credit_r, 1)
+            pl.semaphore_wait(credit_t, 1)
+
+        def kv_step(i, c):
+            h = lax.rem(i + relayed, kv_heads)
             project_kv(h)
-            send_own(parity, h).start()
+
+            @pl.when(h == relayed)
+            def _():
+                hop(parity, 0, 0).start()
+                hop(parity, 0, 1).start()
+
+            @pl.when(h != relayed)
+            def _():
+                send_own(parity, h).start()
 
             @pl.when(jnp.logical_not(odd))
             def _():
@@ -199,9 +245,19 @@
             return c
 
         lax.fori_loop(0, kv_heads, kv_step, 0)
-        flatten_range(layer, 0, q_chunks, True)
+        flatten_range(layer, 0, q_chunks // 2, True)
+        pass_on(parity, 0, 0)
+        flatten_range(layer, q_chunks // 2, q_chunks, True)
 
         def q_step(h, c):
+            @pl.when(h == 1)
+            def _():
+                pass_on(parity, 0, 1)
+
+            @pl.when(h == kv_heads - 1)
+            def _():
+                pass_on(parity, 1, 0)
+
             q = jnp.dot(n_s[...], w_s[h], preferred_element_type=jnp.float32).astype(jnp.bfloat16)
             for g in range(2):
                 for j in range(2):
@@ -210,29 +266,42 @@
 
         lax.fori_loop(0, kv_heads, q_step, 0)
 
-        def attn_step(h, c):
-            slot = lax.rem(h, 2)
-            send_own(parity, h).wait_recv()
+        def attn_step(i, c):
+            slot, h = lax.rem(i, 2), head_at(i)
+
+            @pl.when(i == 1)
+            def _():
+                pass_on(parity, 1, 1)
+
+            per = -(-kv_chunks // (kv_heads - 1))
+            flatten_range(layer + 1, jnp.maximum(i - 1, 0) * per, jnp.minimum(i * per, kv_chunks), False)
+
+            @pl.when(h == relayed)
+            def _():
+                hop(parity, 2, 0).wait_recv()
+                hop(parity, 2, 1).wait_recv()
+
+            @pl.when(h != relayed)
+            def _():
+                send_own(parity, h).wait_recv()
 
             @pl.when(odd)
             def _():
                 send_partner(parity, h, halo_a.at[parity, h]).start()
 
-            flatten_range(layer + 1, h * kv_chunks // kv_heads, (h + 1) * kv_chunks // kv_heads, False)
             send_partner(parity, h, own_s.at[h]).wait_recv()
-            attend(parity, h, 0)
-            attend(parity, h, 1)
-            o_copy(layer, h).wait()
-
-            def out_part(i, cc):
-                cols = pl.ds(pl.multiple_of(i * 512, 512), 512)
+            attend(parity, h)
+            o_copy(layer, i).wait()
+
+            def out_part(t, cc):
+                cols = pl.ds(pl.multiple_of(t * 512, 512), 512)
                 part = jnp.dot(o_s[...], wo_buf[slot, :, cols], preferred_element_type=jnp.float32)
 
-                @pl.when(h == 0)
+                @pl.when(i == 0)
                 def _():
                     acc[:, cols] = part
 
-                @pl.when(h > 0)
+                @pl.when(i > 0)
                 def _():
                     acc[:, cols] = acc[:, cols] + part
 
@@ -240,29 +309,37 @@
 
             lax.fori_loop(0, width // 512, out_part, 0)
 
-            @pl.when(h < kv_heads - 2)
-            def _():
-                o_copy(layer, h + 2).start()
-
-            @pl.when(jnp.logical_and(h >= kv_heads - 2, layer < num_layers - 1))
-            def _():
-                o_copy(layer + 1, h + 2 - kv_heads).start()
+            @pl.when(i < kv_heads - 2)
+            def _():
+                o_copy(layer, i + 2).start()
+
+            @pl.when(jnp.logical_and(i >= kv_heads - 2, layer < num_layers - 1))
+            def _():
+                o_copy(layer + 1, i + 2 - kv_heads).start()
 
             return c
 
         lax.fori_loop(0, kv_heads, attn_step, 0)
 
         def drain(h, c):
-            send_own(parity, h).wait_send()
+            @pl.when(h != relayed)
+            def _():
+                send_own(parity, h).wait_send()
+
             send_partner(parity, h, own_s.at[h]).wait_send()
             return c
 
         lax.fori_loop(0, kv_heads, drain, 0)
+        for leg in range(3):
+            for kv in range(2):
+                hop(parity, leg, kv).wait_send()
 
         @pl.when(layer < num_layers - 2)
         def _():
             pl.semaphore_signal(credit_a, inc=1, device_id={"cp": back}, device_id_type=MESH)
             pl.semaphore_signal(credit_b, inc=1, device_id={"cp": partner}, device_id_type=MESH)
+            pl.semaphore_signal(credit_r, inc=1, device_id={"cp": right}, device_id_type=MESH)
+            pl.semaphore_signal(credit_t, inc=1, device_id={"cp": writer}, device_id_type=MESH)
 
         def update_rows(i, c):
             part = pl.ds(pl.multiple_of(i * 32, 32), 32)
@@ -312,46 +389,68 @@
             pltpu.VMEM((kv_heads, width, 2 * head), bf16),
             pltpu.VMEM((4, 4096, 128), bf16),
             pltpu.VMEM((2, 2 * head, width), bf16),
+            pltpu.VMEM((2, 2, rows, head), bf16),
+            pltpu.VMEM((2, 2, rows, head), bf16),
+            pltpu.VMEM((2 * half, 5 * half), f32),
+            pltpu.VMEM((2 * half, 5 * half), f32),
             dma, dma((4,)), dma((2,)),
-            dma((kv_heads,)), dma((kv_heads,)), dma((2, kv_heads)), dma((2, kv_heads)),
-            pltpu.SemaphoreType.REGULAR, pltpu.SemaphoreType.REGULAR,
+            dma((kv_heads,)), dma((kv_heads,)), dma((2, kv_heads)), dma((2, kv_heads)), dma((3, 2)), dma((2, 3, 2)),
+            pltpu.SemaphoreType.REGULAR, pltpu.SemaphoreType.REGULAR, pltpu.SemaphoreType.REGULAR, pltpu.SemaphoreType.REGULAR,
         ],
         compiler_params=pltpu.CompilerParams(collective_id=0, has_side_effects=True, vmem_limit_bytes=62 * 1024 * 1024),
         name="local_layers",
     )(hidden, tile_rows(w_query), tile_rows(w_key), tile_rows(w_value), w_out, perm_matrix(heads), perm_matrix(kv_heads))
 
 
-def output_kernel(attn, w, x, out, acc):
-    i = pl.program_id(0)
-    part = jnp.dot(attn[...], w[0], preferred_element_type=jnp.float32)
-
-    @pl.when(i == 0)
-    def _():
-        acc[...] = part
-
-    @pl.when(i > 0)
-    def _():
-        acc[...] = acc[...] + part
-
-    @pl.when(i == pl.num_programs(0) - 1)
-    def _():
-        out[...] = (x[...].astype(jnp.float32) + rms_normed(acc[...])).astype(jnp.bfloat16)
-
-
-def output_update(hidden, outs, w_out, layer):
+def partial_kernel(count, *refs):
+    attn, w, out = refs[:count], refs[count], refs[count + 1]
+    for i in range(count):
+        @pl.when(pl.program_id(0) == i)
+        def _(i=i):
+            part = jnp.dot(attn[i][...], w[0], preferred_element_type=jnp.float32)
+            out[...] = part if i == 0 else out[...] + part
+
+
+def final_kernel(attn, w, sofar, x, out, acc):
+    acc[...] = sofar[...] + jnp.dot(attn[...], w[0], preferred_element_type=jnp.float32)
+
+    def one(i, c):
+        part = pl.ds(pl.multiple_of(i * 32, 32), 32)
+        out[part, :] = (x[part, :].astype(jnp.float32) + rms_normed(acc[part, :])).astype(jnp.bfloat16)
+        return c
+
+    lax.fori_loop(0, out.shape[0] // 32, one, 0)
+
+
+def partial_update(outs, w_out, layer):
+    rows, depth = outs[0].shape
+    width = w_out.shape[2]
+    count = len(outs)
+    return pl.pallas_call(
+        functools.partial(partial_kernel, count),
+        grid=(count,),
+        in_specs=[pl.BlockSpec((rows, depth), lambda i: (0, 0))] * count + [pl.BlockSpec((1, depth, width), lambda i: (layer, i, 0))],
+        out_specs=pl.BlockSpec((rows, width), lambda i: (0, 0)),
+        out_shape=jax.ShapeDtypeStruct((rows, width), jnp.float32),
+        cost_estimate=pl.CostEstimate(flops=2 * count * rows * depth * width, bytes_accessed=16_000_000, transcendentals=0),
+        name="partial_update",
+    )(*outs, w_out)
+
+
+def final_update(hidden, sofar, last_out, w_out, layer):
     rows, width = hidden.shape
-    attn = jnp.concatenate(outs, axis=1)
-    depth = attn.shape[1] // 4
+    depth = last_out.shape[1]
+    index = w_out.shape[1] // depth - 1
+    whole = pl.BlockSpec((rows, width), lambda i: (0, 0))
     return pl.pallas_call(
-        output_kernel,
-        grid=(4,),
-        in_specs=[pl.BlockSpec((rows, depth), lambda i: (0, i)), pl.BlockSpec((1, depth, width), lambda i: (layer, i, 0)),
-                  pl.BlockSpec((rows, width), lambda i: (0, 0))],
-        out_specs=pl.BlockSpec((rows, width), lambda i: (0, 0)),
+        final_kernel,
+        grid=(1,),
+        in_specs=[pl.BlockSpec((rows, depth), lambda i: (0, 0)), pl.BlockSpec((1, depth, width), lambda i: (layer, index, 0)), whole, whole],
+        out_specs=whole,
         out_shape=jax.ShapeDtypeStruct((rows, width), jnp.bfloat16),
         scratch_shapes=[pltpu.VMEM((rows, width), jnp.float32)],
-        name="output_update",
-    )(attn, w_out, hidden)
+        name="final_update",
+    )(last_out, w_out, sofar, hidden)
 
 
 def flash_kernel(num_dev, which, q_ref, kv_hbm, out_ref, kv_buf, acc, m_s, l_s, s_a, s_b, sems):
@@ -496,7 +595,7 @@
             for h in range(lo, hi):
                 q = jnp.transpose(queries[:, :, h], (0, 2, 1, 3)).reshape(2, group * half, head)
                 outs.append(flash_head(q, kv_all, h - lo, num_dev))
-        return output_update(hidden, outs, wo, last)
+        return final_update(hidden, partial_update(outs[:-1], wo, last), outs[-1], wo, last)
 
     row_spec = P(("dp", "cp"), None)
     return jax.shard_map(per_device, mesh=mesh, in_specs=(row_spec, P(), P(), P(), P()), out_specs=row_spec, check_vma=False)

time: 651 us -> 654 us (level)
  starting transfers between devices: 9.77 us -> 27.2 us
  Pallas kernels: 398 us -> 383 us
    pallas_call x1, Pallas kernels: 307 us -> 286 us  [local_layers(): pl.pallas_call(functools.partial(local_kernel, num_dev, num_layers), out_...]
    ppermute x1, starting transfers between devices: 3.77 us -> 17.5 us  [to_output_layout(): from_odd = lax.ppermute(hidden[block_len:], 'cp', odd_pairs)]
    ppermute x1, waiting for transfers between devices: 15.6 us -> 5.91 us  [to_output_layout(): from_odd = lax.ppermute(hidden[block_len:], 'cp', odd_pairs)]
    all_gather x1, waiting for transfers between devices: 34.3 us -> 41.2 us  [per_device(): rest = lax.all_gather(kv[cuts[1]:], 'cp')]
    pallas_call x1 -> x2, Pallas kernels: 13.7 us -> 18.9 us  [the longest x1 9.63 us: final_update(): pl.pallas_call(final_kernel, grid=(1,), in_specs=[pl.BlockSpec((rows, dep...]
where the time goes in v3:
time: 654 us; the launch traced here: 649 us
  Pallas kernels  383 us (59%)
  waiting for transfers between devices  195 us (30%)
  starting transfers between devices  27.2 us (4%)
  local copies, waits for them, and re-layouts  19.9 us (3%)
  between operations  13.6 us (2%)
  matrix products  8.41 us (1%)
    pallas_call x1, Pallas kernels, local_layers(): pl.pallas_call(functools.partial(local_kernel, num_dev, num_layers), out_...  286 us
    all_gather x1, waiting for transfers between devices, per_device(): most = lax.all_gather(kv[:cuts[1]], 'cp')  134 us
    pallas_call x4, Pallas kernels, flash_head(): pl.pallas_call(functools.partial(flash_kernel, num_dev, which), out_shape...  77.3 us
    all_gather x1, waiting for transfers between devices, per_device(): rest = lax.all_gather(kv[cuts[1]:], 'cp')  41.2 us
    ppermute x1, starting transfers between devices, to_output_layout(): from_odd = lax.ppermute(hidden[block_len:], 'cp', odd_pairs)  17.5 us
    ppermute x1, waiting for transfers between devices, to_output_layout(): from_even = lax.ppermute(hidden[:block_len], 'cp', even_pairs)  13.9 us
  transfers between devices with their start and end apart: 4, of which 4 were waited for; matrix products, arithmetic and copies ran while one was open for 4% of the time, Pallas kernels for 3%

profile of v3, /device:TPU:127, one launch (start us, length us, event | category | flops | bytes accessed | tf_op | source)
XLA Modules:
  0.0 648.8 jit_solution(17837512241139677607)
XLA Ops:
  6.5 0.0 all-gather.5.cloned.1.call-start
  6.6 286.4 %local_layers.1 = (bf16[512,2560]{1,0:T(8,128)(2,1)}, bf16[4,2,512,256]{3,2,1,0:T(8,128)(2,1)}) custom-call(bf16[512,2560]{1,0:T(8,128)(2,1)} %x_hbm.1, bf16[6,40960,128]{2,1,0:T(8,128)(2,1)} %bitcast.56, bf16[6,20480,128]{2,1,0:T(8,128)(2,1)} %bitcast.57, bf16[6,20480,128]{2,1,0:T(8,128)(2,1)} %bitcast.58, bf16[6,2048,2560]{2,1,0:T(8,128)(2,1)} %bitcast.53, ...), custom_call_target="tpu_custom_call" | custom-call | tf_op jit(solution)/shard_map/local_layers/pallas_call | solution.py:377
  293.0 1.9 slice.31
  294.9 0.1 all-gather.5.cloned.1.call-update
  294.9 0.1 all-gather.7.cloned.1.call-start
  295.0 2.8 slice.33
  297.8 0.1 all-gather.7.cloned.1.call-update
  297.9 0.0 copy-done.4
  297.9 1.8 fusion.9
  299.6 9.6 %collective-permute-start = (bf16[256,2560]{1,0:T(8,128)(2,1)}, bf16[256,2560]{1,0:T(8,128)(2,1)S(1)}, u32[]{:S(2)}, u32[]{:S(2)}) collective-permute-start(bf16[256,2560]{1,0:T(8,128)(2,1)} %get-tuple-element.11), channel_id=1, source_target_pairs={{0,0},{1,2},{2,4},{3,6},{4,8},{5,10},{6,12},{7,14},{8,16},{9,18},{... | collective-permute-start | bytes 3932168 | tf_op jit(solution)/shard_map/ppermute | solution.py:565
  309.2 17.5 %collective-permute-start.1 = (bf16[256,2560]{1,0:T(8,128)(2,1)}, bf16[256,2560]{1,0:T(8,128)(2,1)S(1)}, u32[]{:S(2)}, u32[]{:S(2)}) collective-permute-start(bf16[256,2560]{1,0:T(8,128)(2,1)} %get-tuple-element.12), channel_id=1, source_target_pairs={{0,1},{1,3},{2,5},{3,7},{4,9},{5,11},{6,13},{7,15},{8,17},{9,19},{... | collective-permute-start | bytes 3932168 | tf_op jit(solution)/shard_map/ppermute | solution.py:566
  326.7 10.0 %slice.29 = bf16[1,2560,8,256]{3,2,1,0:T(8,128)(2,1)} slice(bf16[6,2560,8,256]{3,2,1,0:T(8,128)(2,1)} %param.8), slice={[5:6], [0:2560], [0:8], [0:256]} | slice | bytes 20971520 | tf_op jit(solution)/shard_map/slice | solution.py:591
  336.7 13.9 %collective-permute-done = bf16[256,2560]{1,0:T(8,128)(2,1)S(1)} collective-permute-done((bf16[256,2560]{1,0:T(8,128)(2,1)}, bf16[256,2560]{1,0:T(8,128)(2,1)S(1)}, u32[]{:S(2)}, u32[]{:S(2)}) %collective-permute-start) | collective-permute-done | bytes 1310752 | tf_op jit(solution)/shard_map/ppermute | solution.py:565
  350.5 5.9 collective-permute-done.1
  356.4 0.2 broadcast_select_fusion.1
  356.6 0.6 fusion.1
  357.2 8.4 %fusion.6 = bf16[512,8,256]{2,0,1:T(8,128)(2,1)S(1)} fusion(bf16[1,2560,8,256]{3,2,1,0:T(8,128)(2,1)} %slice.29, f32[512]{0:T(512)S(1)} %add_rsqrt_fusion, bf16[256,2560]{1,0:T(8,128)(2,1)S(1)} %get-tuple-element.10, bf16[256,2560]{1,0:T(8,128)(2,1)S(1)} %get-tuple-element.9), kind=kOutput, calls=%fused_computation.9 | convolution fusion | flops 5377622016 | bytes 15206400 | tf_op jit(solution)/shard_map/td,dhe->the/dot_general | solution.py:591
  365.6 0.1 fusion.10
  366.0 1.7 pad_maximum_fusion.x
  367.7 41.2 %all-gather.5.cloned.1.call-done = bf16[32,2,512,256]{3,2,1,0:T(8,128)(2,1)} async-done(((bf16[1,2,512,256]{3,2,1,0:T(8,128)(2,1)}), bf16[32,2,512,256]{3,2,1,0:T(8,128)(2,1)}) %all-gather.5.cloned.1.call-update) | async-done | bytes 16777232 | tf_op jit(solution)/shard_map/all_gather | solution.py:587
  408.9 19.3 %flash_head.4.attn = bf16[512,512]{1,0:T(8,128)(2,1)S(1)} custom-call(bf16[2,512,256]{2,1,0:T(8,128)(2,1)S(1)} %bitcast.52, bf16[32,1,2,512,256]{4,3,2,1,0:T(8,128)(2,1)} %bitcast.63), custom_call_target="tpu_custom_call" | custom-call | flops 20000000000 | bytes 16000000 | tf_op jit(solution)/shard_map/flash_head/pallas_call | solution.py:546
  428.2 0.8 copy-done
  429.0 133.6 %all-gather.7.cloned.1.call-done = bf16[96,2,512,256]{3,2,1,0:T(8,128)(2,1)} async-done(((bf16[3,2,512,256]{3,2,1,0:T(8,128)(2,1)}), bf16[96,2,512,256]{3,2,1,0:T(8,128)(2,1)}) %all-gather.7.cloned.1.call-update) | async-done | bytes 50331664 | tf_op jit(solution)/shard_map/all_gather | solution.py:586
  562.6 19.3 %flash_head.5.refs_0_ = bf16[512,512]{1,0:T(8,128)(2,1)S(1)} custom-call(bf16[2,512,256]{2,1,0:T(8,128)(2,1)S(1)} %bitcast.49, bf16[32,3,2,512,256]{4,3,2,1,0:T(8,128)(2,1)} %bitcast.60), custom_call_target="tpu_custom_call" | custom-call | flops 20000000000 | bytes 16000000 | tf_op jit(solution)/shard_map/flash_head/pallas_call | solution.py:546
  582.0 0.0 copy-start.1
  582.0 0.8 copy-done.1
  582.8 19.3 %flash_head.6.refs_1_ = bf16[512,512]{1,0:T(8,128)(2,1)S(1)} custom-call(bf16[2,512,256]{2,1,0:T(8,128)(2,1)S(1)} %bitcast.50, bf16[32,3,2,512,256]{4,3,2,1,0:T(8,128)(2,1)} %bitcast.61), custom_call_target="tpu_custom_call" | custom-call | flops 20000000000 | bytes 16000000 | tf_op jit(solution)/shard_map/flash_head/pallas_call | solution.py:546
  602.1 0.8 copy-done.2
  602.9 19.3 %flash_head.7.refs_2_ = bf16[512,512]{1,0:T(8,128)(2,1)S(1)} custom-call(bf16[2,512,256]{2,1,0:T(8,128)(2,1)S(1)} %bitcast.51, bf16[32,3,2,512,256]{4,3,2,1,0:T(8,128)(2,1)} %bitcast.62), custom_call_target="tpu_custom_call" | custom-call | flops 20000000000 | bytes 16000000 | tf_op jit(solution)/shard_map/flash_head/pallas_call | solution.py:546
  622.2 0.8 copy-done.3
  623.1 9.3 %partial_update.1.sofar = f32[512,2560]{1,0:T(8,128)} custom-call(bf16[512,512]{1,0:T(8,128)(2,1)} %copy-done.1, bf16[512,512]{1,0:T(8,128)(2,1)} %copy-done.2, bf16[512,512]{1,0:T(8,128)(2,1)} %copy-done.3, bf16[6,2048,2560]{2,1,0:T(8,128)(2,1)} %bitcast.54), custom_call_target="tpu_custom_call" | custom-call | flops 4026531840 | bytes 16000000 | tf_op jit(solution)/shard_map/partial_update/pallas_call | solution.py:429
  632.3 9.6 %final_update.1 = bf16[512,2560]{1,0:T(8,128)(2,1)} custom-call(bf16[512,512]{1,0:T(8,128)(2,1)} %copy-done, bf16[6,2048,2560]{2,1,0:T(8,128)(2,1)} %bitcast.55, f32[512,2560]{1,0:T(8,128)} %partial_update.1.sofar, bf16[512,2560]{1,0:T(8,128)(2,1)} %pad_maximum_fusion.x), custom_call_target="tpu_custom_call" | custom-call | tf_op jit(solution)/shard_map/final_update/pallas_call | solution.py:445
  (9 shorter events, 0.2 us)
Async XLA Ops:
  6.5 402.3 %all-gather.5.cloned.1.call-start = ((), (), s32[]{:S(2)}) async-start(), calls=%async_computation | async-start | bytes 17301504 | tf_op jit(solution)/shard_map/all_gather | solution.py:587
  294.9 3.0 copy-start.4
  294.9 267.7 %all-gather.7.cloned.1.call-start = ((), (), s32[]{:S(2)}) async-start(), calls=%async_computation.1 | async-start | bytes 51904512 | tf_op jit(solution)/shard_map/all_gather | solution.py:586
  299.6 50.9 %collective-permute-start = (bf16[256,2560]{1,0:T(8,128)(2,1)}, bf16[256,2560]{1,0:T(8,128)(2,1)S(1)}, u32[]{:S(2)}, u32[]{:S(2)}) collective-permute-start(bf16[256,2560]{1,0:T(8,128)(2,1)} %get-tuple-element.11), channel_id=1, source_target_pairs={{0,0},{1,2},{2,4},{3,6},{4,8},{5,10},{6,12},{7,14},{8,16},{9,18},{... | collective-permute-start | bytes 3932168 | tf_op jit(solution)/shard_map/ppermute | solution.py:565
  309.2 47.2 %collective-permute-start.1 = (bf16[256,2560]{1,0:T(8,128)(2,1)}, bf16[256,2560]{1,0:T(8,128)(2,1)S(1)}, u32[]{:S(2)}, u32[]{:S(2)}) collective-permute-start(bf16[256,2560]{1,0:T(8,128)(2,1)} %get-tuple-element.12), channel_id=1, source_target_pairs={{0,1},{1,3},{2,5},{3,7},{4,9},{5,11},{6,13},{7,15},{8,17},{9,19},{... | collective-permute-start | bytes 3932168 | tf_op jit(solution)/shard_map/ppermute | solution.py:566
  428.2 0.8 copy-start
  582.0 0.8 copy-start.1
  602.1 0.8 copy-start.2
  622.2 0.8 copy-start.3
Sparse Core Ops, SparseCore 0:
  295.0 113.7 all-gather.4
  411.0 151.6 all-gather.6

commit v4 on v3

--- a/solution.py
+++ b/solution.py
@@ -123,7 +123,8 @@
     def o_copy(layer, i):
         slot = lax.rem(i, 2)
         part = pl.ds(pl.multiple_of(head_at(i) * 2 * head, 2 * head), 2 * head)
-        return pltpu.make_async_copy(wo_hbm.at[layer, part], wo_buf.at[slot], o_sem.at[slot])
+        dst = wo_buf.at[pl.ds(pl.multiple_of(slot * 2 * head, 2 * head), 2 * head)]
+        return pltpu.make_async_copy(wo_hbm.at[layer, part], dst, o_sem.at[slot])
 
     x_copy = pltpu.make_async_copy(x_hbm, x_out, x_sem)
     x_copy.start()
@@ -163,17 +164,17 @@
     x_copy.wait()
 
     def norm_rows(i, carry):
-        part = pl.ds(pl.multiple_of(i * 32, 32), 32)
+        part = pl.ds(pl.multiple_of(i * 64, 64), 64)
         n_s[part, :] = rms_normed(x_out[part, :]).astype(jnp.bfloat16)
         return carry
 
-    lax.fori_loop(0, rows // 32, norm_rows, 0)
+    lax.fori_loop(0, rows // 64, norm_rows, 0)
     flatten_range(0, 0, kv_chunks, False)
 
     bias_a = jnp.where(me < 2, NEG_BIG, 0.0)
     bias_b = jnp.where(me < 1, NEG_BIG, 0.0)
 
-    def attend(parity, h):
+    def attend(parity, h, slot):
         row, key = iota2((half, half), 0), iota2((half, half), 1)
         units = [(j, g, (s_a, s_b)[j].at[g * half:(g + 1) * half]) for j in range(2) for g in range(2)]
 
@@ -208,7 +209,8 @@
                 term = jnp.dot(e.astype(jnp.bfloat16), ref[1, part * half:(part + 1) * half, :], preferred_element_type=jnp.float32)
                 out = term if out is None else out + term
             out = (out / jnp.sum(total, axis=-1, keepdims=True)).astype(jnp.bfloat16)
-            o_s[j * half:(j + 1) * half, g * head:(g + 1) * head] = out
+            cols = pl.ds(pl.multiple_of(slot * 2 * head + g * head, head), head)
+            o_s[j * half:(j + 1) * half, cols] = out
 
     def project_kv(h):
         kv = jnp.dot(n_s[...], w_s[h], preferred_element_type=jnp.float32).astype(jnp.bfloat16)
@@ -245,9 +247,17 @@
             return c
 
         lax.fori_loop(0, kv_heads, kv_step, 0)
-        flatten_range(layer, 0, q_chunks // 2, True)
-        pass_on(parity, 0, 0)
-        flatten_range(layer, q_chunks // 2, q_chunks, True)
+
+        def flatten_q(t, c):
+            flatten_range(layer, t * q_chunks // 2, (t + 1) * q_chunks // 2, True)
+
+            @pl.when(t == 0)
+            def _():
+                pass_on(parity, 0, 0)
+
+            return c
+
+        lax.fori_loop(0, 2, flatten_q, 0)
 
         def q_step(h, c):
             @pl.when(h == 1)
@@ -273,8 +283,8 @@
             def _():
                 pass_on(parity, 1, 1)
 
-            per = -(-kv_chunks // (kv_heads - 1))
-            flatten_range(layer + 1, jnp.maximum(i - 1, 0) * per, jnp.minimum(i * per, kv_chunks), False)
+            early = kv_chunks * 4 // 5
+            flatten_range(layer + 1, jnp.where(i == kv_heads - 1, early, kv_chunks), kv_chunks, False)
 
             @pl.when(h == relayed)
             def _():
@@ -289,33 +299,41 @@
             def _():
                 send_partner(parity, h, halo_a.at[parity, h]).start()
 
+            flatten_range(layer + 1, jnp.minimum(i * early // (kv_heads - 1), early), jnp.minimum((i + 1) * early // (kv_heads - 1), early), False)
             send_partner(parity, h, own_s.at[h]).wait_recv()
-            attend(parity, h)
-            o_copy(layer, i).wait()
-
-            def out_part(t, cc):
-                cols = pl.ds(pl.multiple_of(t * 512, 512), 512)
-                part = jnp.dot(o_s[...], wo_buf[slot, :, cols], preferred_element_type=jnp.float32)
-
-                @pl.when(i == 0)
+            attend(parity, h, slot)
+
+            @pl.when(slot == 1)
+            def _():
+                o_copy(layer, i - 1).wait()
+                o_copy(layer, i).wait()
+                block = width // 2
+
+                def out_part(t, cc):
+                    cols = pl.ds(pl.multiple_of(t * block, block), block)
+                    part = jnp.dot(o_s[...], wo_buf[:, cols], preferred_element_type=jnp.float32)
+
+                    @pl.when(i == 1)
+                    def _():
+                        acc[:, cols] = part
+
+                    @pl.when(i > 1)
+                    def _():
+                        acc[:, cols] = acc[:, cols] + part
+
+                    return cc
+
+                lax.fori_loop(0, 2, out_part, 0)
+
+                @pl.when(i < kv_heads - 2)
                 def _():
-                    acc[:, cols] = part
-
-                @pl.when(i > 0)
+                    o_copy(layer, i + 1).start()
+                    o_copy(layer, i + 2).start()
+
+                @pl.when(jnp.logical_and(i >= kv_heads - 2, layer < num_layers - 1))
                 def _():
-                    acc[:, cols] = acc[:, cols] + part
-
-                return cc
-
-            lax.fori_loop(0, width // 512, out_part, 0)
-
-            @pl.when(i < kv_heads - 2)
-            def _():
-                o_copy(layer, i + 2).start()
-
-            @pl.when(jnp.logical_and(i >= kv_heads - 2, layer < num_layers - 1))
-            def _():
-                o_copy(layer + 1, i + 2 - kv_heads).start()
+                    o_copy(layer + 1, i + 1 - kv_heads).start()
+                    o_copy(layer + 1, i + 2 - kv_heads).start()
 
             return c
 
@@ -342,13 +360,13 @@
             pl.semaphore_signal(credit_t, inc=1, device_id={"cp": writer}, device_id_type=MESH)
 
         def update_rows(i, c):
-            part = pl.ds(pl.multiple_of(i * 32, 32), 32)
+            part = pl.ds(pl.multiple_of(i * 64, 64), 64)
             fresh = (x_out[part, :].astype(jnp.float32) + rms_normed(acc[part, :])).astype(jnp.bfloat16)
             x_out[part, :] = fresh
             n_s[part, :] = rms_normed(fresh).astype(jnp.bfloat16)
             return c
 
-        lax.fori_loop(0, rows // 32, update_rows, 0)
+        lax.fori_loop(0, rows // 64, update_rows, 0)
         return carry
 
     lax.fori_loop(0, num_layers, layer_step, 0)
@@ -384,11 +402,11 @@
             pltpu.VMEM((kv_heads, 2, 2 * half, head), bf16),
             pltpu.VMEM((2, kv_heads, 2, rows, head), bf16),
             pltpu.VMEM((2, kv_heads, 2, rows, head), bf16),
-            pltpu.VMEM((rows, 2 * head), bf16),
+            pltpu.VMEM((rows, 4 * head), bf16),
             pltpu.VMEM((rows, width), f32),
             pltpu.VMEM((kv_heads, width, 2 * head), bf16),
             pltpu.VMEM((4, 4096, 128), bf16),
-            pltpu.VMEM((2, 2 * head, width), bf16),
+            pltpu.VMEM((4 * head, width), bf16),
             pltpu.VMEM((2, 2, rows, head), bf16),
             pltpu.VMEM((2, 2, rows, head), bf16),
             pltpu.VMEM((2 * half, 5 * half), f32),
@@ -415,11 +433,11 @@
     acc[...] = sofar[...] + jnp.dot(attn[...], w[0], preferred_element_type=jnp.float32)
 
     def one(i, c):
-        part = pl.ds(pl.multiple_of(i * 32, 32), 32)
+        part = pl.ds(pl.multiple_of(i * 64, 64), 64)
         out[part, :] = (x[part, :].astype(jnp.float32) + rms_normed(acc[part, :])).astype(jnp.bfloat16)
         return c
 
-    lax.fori_loop(0, out.shape[0] // 32, one, 0)
+    lax.fori_loop(0, out.shape[0] // 64, one, 0)
 
 
 def partial_update(outs, w_out, layer):

time: 654 us -> 644 us (0.985)
  Pallas kernels: 383 us -> 375 us
    ppermute x1, starting transfers between devices: 17.5 us -> 10.1 us  [to_output_layout(): from_odd = lax.ppermute(hidden[block_len:], 'cp', odd_pairs)]
    pallas_call x1, Pallas kernels: 286 us -> 279 us  [local_layers(): pl.pallas_call(functools.partial(local_kernel, num_dev, num_layers), out_...]
where the time goes in v4:
time: 644 us; the launch traced here: 639 us
  Pallas kernels  375 us (58%)
  waiting for transfers between devices  195 us (30%)
  starting transfers between devices  24.8 us (4%)
  local copies, waits for them, and re-layouts  19.9 us (3%)
  between operations  13.6 us (2%)
  matrix products  8.41 us (1%)
    pallas_call x1, Pallas kernels, local_layers(): pl.pallas_call(functools.partial(local_kernel, num_dev, num_layers), out_...  279 us
    all_gather x1, waiting for transfers between devices, per_device(): most = lax.all_gather(kv[:cuts[1]], 'cp')  134 us
    pallas_call x4, Pallas kernels, flash_head(): pl.pallas_call(functools.partial(flash_kernel, num_dev, which), out_shape...  77.3 us
    all_gather x1, waiting for transfers between devices, per_device(): rest = lax.all_gather(kv[cuts[1]:], 'cp')  43.7 us
    ppermute x1, starting transfers between devices, to_output_layout(): from_even = lax.ppermute(hidden[:block_len], 'cp', even_pairs)  14.6 us
    ppermute x1, waiting for transfers between devices, to_output_layout(): from_even = lax.ppermute(hidden[:block_len], 'cp', even_pairs)  13.9 us
  transfers between devices with their start and end apart: 4, of which 4 were waited for; matrix products, arithmetic and copies ran while one was open for 4% of the time, Pallas kernels for 3%

profile of v4, /device:TPU:127, one launch (start us, length us, event | category | flops | bytes accessed | tf_op | source)
XLA Modules:
  0.0 638.5 jit_solution(1422871788485659161)
XLA Ops:
  6.5 0.0 all-gather.5.cloned.1.call-start
  6.6 279.3 %local_layers.1 = (bf16[512,2560]{1,0:T(8,128)(2,1)}, bf16[4,2,512,256]{3,2,1,0:T(8,128)(2,1)}) custom-call(bf16[512,2560]{1,0:T(8,128)(2,1)} %x_hbm.1, bf16[6,40960,128]{2,1,0:T(8,128)(2,1)} %bitcast.56, bf16[6,20480,128]{2,1,0:T(8,128)(2,1)} %bitcast.57, bf16[6,20480,128]{2,1,0:T(8,128)(2,1)} %bitcast.58, bf16[6,2048,2560]{2,1,0:T(8,128)(2,1)} %bitcast.53, ...), custom_call_target="tpu_custom_call" | custom-call | tf_op jit(solution)/shard_map/local_layers/pallas_call | solution.py:395
  285.8 1.9 slice.31
  287.7 0.1 all-gather.5.cloned.1.call-update
  287.8 0.1 all-gather.7.cloned.1.call-start
  287.9 2.8 slice.33
  290.7 0.1 all-gather.7.cloned.1.call-update
  290.7 0.0 copy-done.4
  290.7 1.8 fusion.9
  292.5 14.6 %collective-permute-start = (bf16[256,2560]{1,0:T(8,128)(2,1)}, bf16[256,2560]{1,0:T(8,128)(2,1)S(1)}, u32[]{:S(2)}, u32[]{:S(2)}) collective-permute-start(bf16[256,2560]{1,0:T(8,128)(2,1)} %get-tuple-element.11), channel_id=1, source_target_pairs={{0,0},{1,2},{2,4},{3,6},{4,8},{5,10},{6,12},{7,14},{8,16},{9,18},{... | collective-permute-start | bytes 3932168 | tf_op jit(solution)/shard_map/ppermute | solution.py:583
  307.2 10.1 %collective-permute-start.1 = (bf16[256,2560]{1,0:T(8,128)(2,1)}, bf16[256,2560]{1,0:T(8,128)(2,1)S(1)}, u32[]{:S(2)}, u32[]{:S(2)}) collective-permute-start(bf16[256,2560]{1,0:T(8,128)(2,1)} %get-tuple-element.12), channel_id=1, source_target_pairs={{0,1},{1,3},{2,5},{3,7},{4,9},{5,11},{6,13},{7,15},{8,17},{9,19},{... | collective-permute-start | bytes 3932168 | tf_op jit(solution)/shard_map/ppermute | solution.py:584
  317.2 9.9 %slice.29 = bf16[1,2560,8,256]{3,2,1,0:T(8,128)(2,1)} slice(bf16[6,2560,8,256]{3,2,1,0:T(8,128)(2,1)} %param.8), slice={[5:6], [0:2560], [0:8], [0:256]} | slice | bytes 20971520 | tf_op jit(solution)/shard_map/slice | solution.py:609
  327.2 13.9 %collective-permute-done = bf16[256,2560]{1,0:T(8,128)(2,1)S(1)} collective-permute-done((bf16[256,2560]{1,0:T(8,128)(2,1)}, bf16[256,2560]{1,0:T(8,128)(2,1)S(1)}, u32[]{:S(2)}, u32[]{:S(2)}) %collective-permute-start) | collective-permute-done | bytes 1310752 | tf_op jit(solution)/shard_map/ppermute | solution.py:583
  341.0 3.5 collective-permute-done.1
  344.5 0.2 broadcast_select_fusion.1
  344.6 0.6 fusion.1
  345.2 8.4 %fusion.6 = bf16[512,8,256]{2,0,1:T(8,128)(2,1)S(1)} fusion(bf16[1,2560,8,256]{3,2,1,0:T(8,128)(2,1)} %slice.29, f32[512]{0:T(512)S(1)} %add_rsqrt_fusion, bf16[256,2560]{1,0:T(8,128)(2,1)S(1)} %get-tuple-element.10, bf16[256,2560]{1,0:T(8,128)(2,1)S(1)} %get-tuple-element.9), kind=kOutput, calls=%fused_computation.9 | convolution fusion | flops 5377622016 | bytes 15206400 | tf_op jit(solution)/shard_map/td,dhe->the/dot_general | solution.py:609
  353.7 0.1 fusion.10
  354.0 1.7 pad_maximum_fusion.x
  355.7 43.7 %all-gather.5.cloned.1.call-done = bf16[32,2,512,256]{3,2,1,0:T(8,128)(2,1)} async-done(((bf16[1,2,512,256]{3,2,1,0:T(8,128)(2,1)}), bf16[32,2,512,256]{3,2,1,0:T(8,128)(2,1)}) %all-gather.5.cloned.1.call-update) | async-done | bytes 16777232 | tf_op jit(solution)/shard_map/all_gather | solution.py:605
  399.4 19.3 %flash_head.4.attn = bf16[512,512]{1,0:T(8,128)(2,1)S(1)} custom-call(bf16[2,512,256]{2,1,0:T(8,128)(2,1)S(1)} %bitcast.52, bf16[32,1,2,512,256]{4,3,2,1,0:T(8,128)(2,1)} %bitcast.63), custom_call_target="tpu_custom_call" | custom-call | flops 20000000000 | bytes 16000000 | tf_op jit(solution)/shard_map/flash_head/pallas_call | solution.py:564
  418.7 0.8 copy-done
  419.5 133.6 %all-gather.7.cloned.1.call-done = bf16[96,2,512,256]{3,2,1,0:T(8,128)(2,1)} async-done(((bf16[3,2,512,256]{3,2,1,0:T(8,128)(2,1)}), bf16[96,2,512,256]{3,2,1,0:T(8,128)(2,1)}) %all-gather.7.cloned.1.call-update) | async-done | bytes 50331664 | tf_op jit(solution)/shard_map/all_gather | solution.py:604
  553.1 19.3 %flash_head.5.refs_0_ = bf16[512,512]{1,0:T(8,128)(2,1)S(1)} custom-call(bf16[2,512,256]{2,1,0:T(8,128)(2,1)S(1)} %bitcast.49, bf16[32,3,2,512,256]{4,3,2,1,0:T(8,128)(2,1)} %bitcast.60), custom_call_target="tpu_custom_call" | custom-call | flops 20000000000 | bytes 16000000 | tf_op jit(solution)/shard_map/flash_head/pallas_call | solution.py:564
  572.5 0.0 copy-start.1
  572.5 0.8 copy-done.1
  573.3 19.3 %flash_head.6.refs_1_ = bf16[512,512]{1,0:T(8,128)(2,1)S(1)} custom-call(bf16[2,512,256]{2,1,0:T(8,128)(2,1)S(1)} %bitcast.50, bf16[32,3,2,512,256]{4,3,2,1,0:T(8,128)(2,1)} %bitcast.61), custom_call_target="tpu_custom_call" | custom-call | flops 20000000000 | bytes 16000000 | tf_op jit(solution)/shard_map/flash_head/pallas_call | solution.py:564
  592.6 0.8 copy-done.2
  593.4 19.3 %flash_head.7.refs_2_ = bf16[512,512]{1,0:T(8,128)(2,1)S(1)} custom-call(bf16[2,512,256]{2,1,0:T(8,128)(2,1)S(1)} %bitcast.51, bf16[32,3,2,512,256]{4,3,2,1,0:T(8,128)(2,1)} %bitcast.62), custom_call_target="tpu_custom_call" | custom-call | flops 20000000000 | bytes 16000000 | tf_op jit(solution)/shard_map/flash_head/pallas_call | solution.py:564
  612.7 0.8 copy-done.3
  613.5 9.3 %partial_update.1.sofar = f32[512,2560]{1,0:T(8,128)} custom-call(bf16[512,512]{1,0:T(8,128)(2,1)} %copy-done.1, bf16[512,512]{1,0:T(8,128)(2,1)} %copy-done.2, bf16[512,512]{1,0:T(8,128)(2,1)} %copy-done.3, bf16[6,2048,2560]{2,1,0:T(8,128)(2,1)} %bitcast.54), custom_call_target="tpu_custom_call" | custom-call | flops 4026531840 | bytes 16000000 | tf_op jit(solution)/shard_map/partial_update/pallas_call | solution.py:447
  622.8 8.9 %final_update.1 = bf16[512,2560]{1,0:T(8,128)(2,1)} custom-call(bf16[512,512]{1,0:T(8,128)(2,1)} %copy-done, bf16[6,2048,2560]{2,1,0:T(8,128)(2,1)} %bitcast.55, f32[512,2560]{1,0:T(8,128)} %partial_update.1.sofar, bf16[512,2560]{1,0:T(8,128)(2,1)} %pad_maximum_fusion.x), custom_call_target="tpu_custom_call" | custom-call | tf_op jit(solution)/shard_map/final_update/pallas_call | solution.py:463
  (9 shorter events, 0.2 us)
Async XLA Ops:
  6.5 392.8 %all-gather.5.cloned.1.call-start = ((), (), s32[]{:S(2)}) async-start(), calls=%async_computation | async-start | bytes 17301504 | tf_op jit(solution)/shard_map/all_gather | solution.py:605
  287.7 3.0 copy-start.4
  287.8 265.3 %all-gather.7.cloned.1.call-start = ((), (), s32[]{:S(2)}) async-start(), calls=%async_computation.1 | async-start | bytes 51904512 | tf_op jit(solution)/shard_map/all_gather | solution.py:604
  292.5 48.5 %collective-permute-start = (bf16[256,2560]{1,0:T(8,128)(2,1)}, bf16[256,2560]{1,0:T(8,128)(2,1)S(1)}, u32[]{:S(2)}, u32[]{:S(2)}) collective-permute-start(bf16[256,2560]{1,0:T(8,128)(2,1)} %get-tuple-element.11), channel_id=1, source_target_pairs={{0,0},{1,2},{2,4},{3,6},{4,8},{5,10},{6,12},{7,14},{8,16},{9,18},{... | collective-permute-start | bytes 3932168 | tf_op jit(solution)/shard_map/ppermute | solution.py:583
  307.2 37.3 %collective-permute-start.1 = (bf16[256,2560]{1,0:T(8,128)(2,1)}, bf16[256,2560]{1,0:T(8,128)(2,1)S(1)}, u32[]{:S(2)}, u32[]{:S(2)}) collective-permute-start(bf16[256,2560]{1,0:T(8,128)(2,1)} %get-tuple-element.12), channel_id=1, source_target_pairs={{0,1},{1,3},{2,5},{3,7},{4,9},{5,11},{6,13},{7,15},{8,17},{9,19},{... | collective-permute-start | bytes 3932168 | tf_op jit(solution)/shard_map/ppermute | solution.py:584
  418.7 0.8 copy-start
  572.5 0.8 copy-start.1
  592.6 0.8 copy-start.2
  612.7 0.8 copy-start.3
Sparse Core Ops, SparseCore 0:
  287.9 111.3 all-gather.4
  401.4 151.6 all-gather.6
